TPU v7x, 32 devices: a whole 2x2x4 slice. The times are simulated.
32 devices in a mesh: section: 4 (over y, core), expert: 8 (over z, x).
Axes of the slice: x: 2, y: 2, z: 4, core: 2. Of those that a mesh axis runs over, the one named last changes fastest.
Arguments:
- pending_inputs: bfloat16 [4, 256, 4096], P('section', 'expert'), may hold values from -6 to 6
- arriving_microgroups: bfloat16 [1, 256, 4096], P(None, 'expert'), may hold values from -6 to 6
- expert_assignment: int32 [4, 2, 256, 2], P('section', None, 'expert'), may hold values from 0 to 3, all different within a row; in each aligned block of 32 rows (0 to 31, 32 to 63, ..., all dimensions but the last counted through in order) at most 24 rows name the same one
- segment_rescale_factor: float32 [4, 4096], P('section'), may hold values from 0.5 to 1.5
- assignment_logit_maps: float32 [4, 4096, 4], P('section'), may hold values from -0.09375 to 0.09375
- gating_projections: bfloat16 [4, 4096, 28672], P('section', None, 'expert'), may hold values from -0.09375 to 0.09375
- expanding_projections: bfloat16 [4, 4096, 28672], P('section', None, 'expert'), may hold values from -0.09375 to 0.09375
- contracting_projections: bfloat16 [4, 28672, 4096], P('section', 'expert'), may hold values from -0.0625 to 0.0625
Outputs:
- carried: bfloat16 [2, 4, 256, 4096], P(None, 'section', 'expert')
Inputs may be any that keep to these rules, and one draw needn't show every extreme that they name: `expert_assignment`: the two experts of a row differ. Among the rows of one device (one section, one step, 32 tokens), no expert is named more than 24 times, and in every draw some expert is named exactly 24 times.
All inputs are finite; a program needn't handle non-finite values.
Results may differ from a plain program's by a relative error of at most 0.0085.
Values may be sent and summed in bfloat16 or wider, within the bound.
No kernel may reach another device: no remote copies, remote signals or barrier semaphores. Data moves between devices by JAX's collectives and lax.ppermute only.
A program may use at most 128 MiB of HBM per device.

v0:
```python
import jax
import jax.numpy as jnp
from jax import lax
from jax.sharding import PartitionSpec as P

EXPERTS = 4
STEPS = 2
CAP = 24


epsilon = 1e-05


def shifted(x, axis, by):
    size = lax.axis_size(axis)
    return lax.ppermute(x, axis, [(i, (i + by) % size) for i in range(size)])


def expert_rows(token_rows, gate_cols, up_cols, down_rows):
    matrix = token_rows.reshape(-1, token_rows.shape[-1])
    gate_value = jnp.dot(matrix, gate_cols, preferred_element_type=jnp.float32)
    up_value = jnp.dot(matrix, up_cols, preferred_element_type=jnp.float32)
    hidden = (jax.nn.silu(gate_value) * up_value).astype(jnp.bfloat16)
    output = jnp.dot(hidden, down_rows, preferred_element_type=jnp.float32)
    return output.reshape(token_rows.shape[0], token_rows.shape[1], -1)


def route_slots(chosen):
    chosen_flat = chosen.reshape(-1)
    expert_hits = (chosen_flat[:, None] == jnp.arange(EXPERTS, dtype=jnp.int32)[None, :]).astype(
        jnp.int32
    )
    before = jnp.cumsum(expert_hits, 0) - expert_hits
    position = jnp.sum(before * expert_hits, 1)
    return chosen_flat * CAP + position


def moe_layer(
    activation,
    chosen,
    segment_rescale_factor,
    assignment_logit_maps,
    gate_cols,
    up_cols,
    down_rows,
    group_size,
):
    as_float = activation.astype(jnp.float32)
    normed = (
        as_float
        * lax.rsqrt(jnp.mean(as_float * as_float, -1, keepdims=True) + epsilon)
        * segment_rescale_factor
    ).astype(jnp.bfloat16)
    logits = jnp.dot(
        normed.astype(jnp.float32), assignment_logit_maps, precision=lax.Precision.HIGHEST
    )
    chooses = chosen[:, :, None] == jnp.arange(EXPERTS, dtype=jnp.int32)[None, None, :]
    picked = jnp.sum(jnp.where(chooses, logits[:, None, :], 0.0), -1)
    first_share = jax.nn.sigmoid(picked[:, 0] - picked[:, 1])
    share_pair = jnp.stack([first_share, 1.0 - first_share], 1).astype(jnp.bfloat16)
    model_width = activation.shape[-1]
    slot_index = route_slots(chosen)
    places = jnp.arange(EXPERTS * CAP, dtype=jnp.int32)
    selector = (places[:, None] == slot_index[None, :]).astype(jnp.bfloat16)
    doubled = jnp.repeat(normed, 2, axis=0)
    routed = jnp.dot(selector, doubled, preferred_element_type=jnp.float32).astype(jnp.bfloat16)
    copies = jnp.broadcast_to(
        routed.reshape(EXPERTS, 1, CAP, model_width), (EXPERTS, group_size, CAP, model_width)
    )
    copies = copies.reshape(EXPERTS * group_size, CAP, model_width)
    partial_value = expert_rows(
        lax.all_to_all(copies, "expert", split_axis=0, concat_axis=0, tiled=True),
        gate_cols,
        up_cols,
        down_rows,
    )
    returned = lax.all_to_all(partial_value, "expert", split_axis=0, concat_axis=0, tiled=True)
    expert_out = jnp.sum(returned.reshape(EXPERTS, group_size, CAP, model_width), 1).reshape(
        EXPERTS * CAP, model_width
    )
    combiner = jnp.where(
        slot_index[:, None] == places[None, :],
        share_pair.reshape(-1).astype(jnp.float32)[:, None],
        0.0,
    )
    mixture = jnp.dot(combiner, expert_out, precision=lax.Precision.HIGHEST)
    mixture = jnp.sum(mixture.reshape(activation.shape[0], 2, model_width), 1)
    return (as_float + mixture).astype(jnp.bfloat16)


def shards(
    pending_inputs,
    arriving_microgroups,
    expert_assignment,
    segment_rescale_factor,
    assignment_logit_maps,
    gating_projections,
    expanding_projections,
    contracting_projections,
):
    section_index = lax.axis_index("section")
    group_size = lax.axis_size("expert") // EXPERTS
    present_activation = pending_inputs[0]
    records = []
    for step_index in range(STEPS):
        if step_index > 0:
            present_activation = jnp.where(
                section_index == 0, arriving_microgroups[step_index - 1], present_activation
            )
        result = moe_layer(
            present_activation,
            expert_assignment[0, step_index],
            segment_rescale_factor[0],
            assignment_logit_maps[0],
            gating_projections[0],
            expanding_projections[0],
            contracting_projections[0],
            group_size,
        )
        present_activation = shifted(result, "section", 1)
        records.append(present_activation)
    return jnp.stack(records)[:, None]


def solution(mesh):
    return jax.shard_map(
        shards,
        mesh=mesh,
        in_specs=(
            P("section", "expert", None),
            P(None, "expert", None),
            P("section", None, "expert", None),
            P("section", None),
            P("section", None, None),
            P("section", None, "expert"),
            P("section", None, "expert"),
            P("section", "expert", None),
        ),
        out_specs=P(None, "section", "expert", None),
        check_vma=False,
    )
```

profile of v0, /device:TPU:0, one launch (start us, length us, event | category | flops | bytes accessed | tf_op | source)
XLA Modules:
  0.0 333.3 jit_solution(4239723911729603645)
XLA Ops:
  0.0 0.0 copy-start
  0.0 1.1 fusion.27
  1.2 0.0 copy-start.10
  1.2 1.3 slice_bitcast_fusion
  2.4 0.1 copy.25
  2.5 0.1 eq.139
  2.6 0.1 fusion.50
  2.7 0.1 reduce_window_sum.17
  2.8 0.2 select_reduce_fusion.1
  3.0 1.1 fusion.29
  4.1 0.5 broadcast_in_dim.81
  4.6 0.2 reshape.190
  4.8 0.3 convolution_convert_fusion.1
  5.1 0.2 broadcast_in_dim.83
  5.3 0.0 copy-done.10
  5.3 44.1 %all_to_all.20 = bf16[8,24,4096]{2,1,0:T(8,128)(2,1)S(1)} all-to-all(bf16[8,24,4096]{2,1,0:T(8,128)(2,1)S(1)} %bitcast.101), channel_id=1, replica_groups=mesh['section'=4,'expert'=8] {'expert'}, dimensions={0} | all-to-all | bytes 3145728 | tf_op jit(solution)/shard_map/all_to_all | solution.py:72
  49.4 12.4 %fusion.10 = f32[192,3584]{1,0:T(8,128)S(1)} fusion(bf16[192,4096]{1,0:T(8,128)(2,1)S(1)} %bitcast.107, bf16[1,4096,3584]{2,1,0:T(8,128)(2,1)} %param.13), kind=kOutput, calls=%fused_computation.10 | convolution fusion | flops 5637144576 | bytes 33685504 | tf_op jit(solution)/shard_map/dot_general | solution.py:21
  61.8 12.5 %fusion.21 = bf16[192,3584]{1,0:T(8,128)(2,1)S(1)} fusion(bf16[192,4096]{1,0:T(8,128)(2,1)S(1)} %bitcast.108, bf16[1,4096,3584]{2,1,0:T(8,128)(2,1)} %param.14, f32[192,3584]{1,0:T(8,128)S(1)} %fusion.10), kind=kOutput, calls=%fused_computation.15 | convolution fusion | flops 5641273344 | bytes 35061760 | tf_op jit(solution)/shard_map/dot_general | solution.py:22
  74.3 14.1 %fusion.2 = f32[8,24,4096]{2,1,0:T(8,128)} fusion(bf16[8,24,3584]{2,1,0:T(8,128)(2,1)S(1)} %bitcast.116, bf16[1,3584,4096]{2,1,0:T(8,128)(2,1)} %param.15), kind=kOutput, calls=%fused_computation.2 | convolution fusion | flops 5637144576 | bytes 33882112 | tf_op jit(solution)/shard_map/dot_general | solution.py:24
  88.4 3.8 %all-to-all-start.1 = ((f32[8,24,4096]{2,1,0:T(8,128)}), f32[8,24,4096]{2,1,0:T(8,128)S(1)}, u32[]{:S(2)}, u32[]{:S(2)}) async-start(f32[8,24,4096]{2,1,0:T(8,128)} %fusion.2), calls=%async_computation.1 | async-start | bytes 6291456 | tf_op jit(solution)/shard_map/all_to_all | solution.py:77
  92.2 0.1 reduce_sum.95
  92.3 0.1 copy.27
  92.4 0.7 eq.153
  93.1 0.7 copy.26
  93.8 0.8 fusion.48
  94.5 0.1 reduce_window_sum.18
  94.6 0.9 select_reduce_fusion
  95.5 0.1 reduce_sum.101
  95.6 0.1 copy.28
  95.7 0.0 copy-done
  95.7 0.0 copy-done.1
  95.7 0.0 copy-done.7
  95.7 1.0 fusion.38
  96.7 0.7 select_reduce_fusion.3
  97.4 0.7 multiply_add_fusion
  98.1 64.3 %all-to-all-done.1 = f32[8,24,4096]{2,1,0:T(8,128)S(1)} async-done(((f32[8,24,4096]{2,1,0:T(8,128)}), f32[8,24,4096]{2,1,0:T(8,128)S(1)}, u32[]{:S(2)}, u32[]{:S(2)}) %all-to-all-start.1) | async-done | bytes 3145760 | tf_op jit(solution)/shard_map/all_to_all | solution.py:77
  162.4 0.2 bitcast_reduce_fusion.1
  162.7 0.0 copy-start.8
  162.7 0.0 copy-start.6
  162.7 1.2 convolution_reduce_fusion.1
  164.0 0.2 collective-permute-start
  164.2 0.0 copy-done.8
  164.2 5.8 %collective-permute-done = bf16[32,4096]{1,0:T(8,128)(2,1)S(1)} collective-permute-done((bf16[32,4096]{1,0:T(8,128)(2,1)S(1)}, bf16[32,4096]{1,0:T(8,128)(2,1)S(1)}, u32[]{:S(2)}, u32[]{:S(2)}) %collective-permute-start) | collective-permute-done | bytes 262176 | tf_op jit(solution)/shard_map/ppermute | solution.py:16
  170.0 0.2 fusion.33
  170.2 0.7 copy-done.2
  170.9 0.1 fusion.35
  171.0 0.5 broadcast_in_dim.86
  171.5 0.2 reshape.195
  171.7 0.3 convolution_convert_fusion
  172.1 0.2 broadcast_in_dim.88
  172.3 39.9 %all_to_all.21 = bf16[8,24,4096]{2,1,0:T(8,128)(2,1)S(1)} all-to-all(bf16[8,24,4096]{2,1,0:T(8,128)(2,1)S(1)} %bitcast.102), channel_id=1, replica_groups=mesh['section'=4,'expert'=8] {'expert'}, dimensions={0} | all-to-all | bytes 3145728 | tf_op jit(solution)/shard_map/all_to_all | solution.py:72
  212.1 12.4 %fusion.8 = f32[192,3584]{1,0:T(8,128)S(1)} fusion(bf16[192,4096]{1,0:T(8,128)(2,1)S(1)} %bitcast.109, bf16[1,4096,3584]{2,1,0:T(8,128)(2,1)} %param.13), kind=kOutput, calls=%fused_computation.8 | convolution fusion | flops 5637144576 | bytes 33685504 | tf_op jit(solution)/shard_map/dot_general | solution.py:21
  224.5 12.5 %fusion.18 = bf16[192,3584]{1,0:T(8,128)(2,1)S(1)} fusion(bf16[192,4096]{1,0:T(8,128)(2,1)S(1)} %bitcast.110, bf16[1,4096,3584]{2,1,0:T(8,128)(2,1)} %param.14, f32[192,3584]{1,0:T(8,128)S(1)} %fusion.8), kind=kOutput, calls=%fused_computation.14 | convolution fusion | flops 5641273344 | bytes 35061760 | tf_op jit(solution)/shard_map/dot_general | solution.py:22
  237.0 14.1 %fusion = f32[8,24,4096]{2,1,0:T(8,128)} fusion(bf16[8,24,3584]{2,1,0:T(8,128)(2,1)S(1)} %bitcast.117, bf16[1,3584,4096]{2,1,0:T(8,128)(2,1)} %param.15), kind=kOutput, calls=%fused_computation | convolution fusion | flops 5637144576 | bytes 33882112 | tf_op jit(solution)/shard_map/dot_general | solution.py:24
  251.1 3.8 %all-to-all-start.3 = ((f32[8,24,4096]{2,1,0:T(8,128)}), f32[8,24,4096]{2,1,0:T(8,128)S(1)}, u32[]{:S(2)}, u32[]{:S(2)}) async-start(f32[8,24,4096]{2,1,0:T(8,128)} %fusion), calls=%async_computation.3 | async-start | bytes 6291456 | tf_op jit(solution)/shard_map/all_to_all | solution.py:77
  254.9 0.3 fusion.42
  255.3 0.0 copy-start.3
  255.3 69.8 %all-to-all-done.3 = f32[8,24,4096]{2,1,0:T(8,128)S(1)} async-done(((f32[8,24,4096]{2,1,0:T(8,128)}), f32[8,24,4096]{2,1,0:T(8,128)S(1)}, u32[]{:S(2)}, u32[]{:S(2)}) %all-to-all-start.3) | async-done | bytes 3145760 | tf_op jit(solution)/shard_map/all_to_all | solution.py:77
  325.1 0.2 bitcast_reduce_fusion
  325.3 1.2 convolution_reduce_fusion
  326.6 0.1 collective-permute-start.1
  326.7 5.8 %collective-permute-done.1 = bf16[32,4096]{1,0:T(8,128)(2,1)S(1)} collective-permute-done((bf16[32,4096]{1,0:T(8,128)(2,1)S(1)}, bf16[32,4096]{1,0:T(8,128)(2,1)S(1)}, u32[]{:S(2)}, u32[]{:S(2)}) %collective-permute-start.1) | collective-permute-done | bytes 262176 | tf_op jit(solution)/shard_map/ppermute | solution.py:16
  332.4 0.0 copy-done.5
  332.4 0.8 maximum_bitcast_fusion
  (23 shorter events, 0.2 us)
Async XLA Ops:
  0.0 95.7 %copy-start = (f32[1,4096,4]{1,2,0:T(4,128)S(1)}, f32[1,4096,4]{1,2,0:T(4,128)}, u32[]{:S(2)}) copy-start(f32[1,4096,4]{1,2,0:T(4,128)} %param.12) | copy-start | bytes 196612
  1.2 4.1 %copy-start.10 = (f32[32]{0:T(128)}, f32[32]{0:T(128)S(1)}, u32[]{:S(2)}) copy-start(f32[32]{0:T(128)S(1)} %add_rsqrt_fusion.1) | copy-start | bytes 388
  88.4 7.3 %copy-start.1 = (bf16[1,32,4096]{2,1,0:T(8,128)(2,1)S(1)}, bf16[1,32,4096]{2,1,0:T(8,128)(2,1)}, u32[]{:S(2)}) copy-start(bf16[1,32,4096]{2,1,0:T(8,128)(2,1)} %param.8) | copy-start | bytes 786436
  88.4 7.3 %copy-start.7 = (f32[1,4096]{1,0:T(1,128)S(1)}, f32[1,4096]{1,0:T(1,128)}, u32[]{:S(2)}) copy-start(f32[1,4096]{1,0:T(1,128)} %param.11) | copy-start | bytes 49156
  88.4 74.0 %all-to-all-start.1 = ((f32[8,24,4096]{2,1,0:T(8,128)}), f32[8,24,4096]{2,1,0:T(8,128)S(1)}, u32[]{:S(2)}, u32[]{:S(2)}) async-start(f32[8,24,4096]{2,1,0:T(8,128)} %fusion.2), calls=%async_computation.1 | async-start | bytes 6291456 | tf_op jit(solution)/shard_map/all_to_all | solution.py:77
  162.7 1.5 copy-start.8
  162.7 7.3 %copy-start.6 = (bf16[1,32,4096]{2,1,0:T(8,128)(2,1)S(1)}, bf16[1,32,4096]{2,1,0:T(8,128)(2,1)}, u32[]{:S(2)}) copy-start(bf16[1,32,4096]{2,1,0:T(8,128)(2,1)} %param.9) | copy-start | bytes 786436
  164.0 6.0 %collective-permute-start = (bf16[32,4096]{1,0:T(8,128)(2,1)S(1)}, bf16[32,4096]{1,0:T(8,128)(2,1)S(1)}, u32[]{:S(2)}, u32[]{:S(2)}) collective-permute-start(bf16[32,4096]{1,0:T(8,128)(2,1)S(1)} %fusion.30), channel_id=1, source_target_pairs={{0,8},{8,16},{16,24},{24,0},{1,9},{9,17},{17,25},{25,1},{2,10},{10... | collective-permute-start | bytes 786440 | tf_op jit(solution)/shard_map/ppermute | solution.py:16
  170.0 1.1 copy-start.4
  170.2 0.7 copy-start.2
  251.1 4.1 %copy-start.9 = (s32[32,2]{0,1:T(2,128)S(1)}, s32[32,2]{0,1:T(2,128)}, u32[]{:S(2)}) copy-start(s32[32,2]{0,1:T(2,128)} %get-tuple-element.13) | copy-start | bytes 772
  251.1 74.0 %all-to-all-start.3 = ((f32[8,24,4096]{2,1,0:T(8,128)}), f32[8,24,4096]{2,1,0:T(8,128)S(1)}, u32[]{:S(2)}, u32[]{:S(2)}) async-start(f32[8,24,4096]{2,1,0:T(8,128)} %fusion), calls=%async_computation.3 | async-start | bytes 6291456 | tf_op jit(solution)/shard_map/all_to_all | solution.py:77
  255.3 71.2 %copy-start.3 = (bf16[32,4096]{1,0:T(8,128)(2,1)S(1)}, bf16[32,4096]{1,0:T(8,128)(2,1)}, u32[]{:S(2)}) copy-start(bf16[32,4096]{1,0:T(8,128)(2,1)} %copy-done.2) | copy-start | bytes 786436
  325.3 7.1 %copy-start.5 = (bf16[32,4096]{1,0:T(8,128)(2,1)S(1)}, bf16[32,4096]{1,0:T(8,128)(2,1)}, u32[]{:S(2)}) copy-start(bf16[32,4096]{1,0:T(8,128)(2,1)} %copy-done.4) | copy-start | bytes 786436
  326.6 5.8 %collective-permute-start.1 = (bf16[32,4096]{1,0:T(8,128)(2,1)S(1)}, bf16[32,4096]{1,0:T(8,128)(2,1)S(1)}, u32[]{:S(2)}, u32[]{:S(2)}) collective-permute-start(bf16[32,4096]{1,0:T(8,128)(2,1)S(1)} %fusion.36), channel_id=1, source_target_pairs={{0,8},{8,16},{16,24},{24,0},{1,9},{9,17},{17,25},{25,1},{2,10},{10... | collective-permute-start | bytes 786440 | tf_op jit(solution)/shard_map/ppermute | solution.py:16
where the time goes:
time: 334 us; the launch traced here: 333 us
  waiting for transfers between devices  146 us (44%)
  blocking collectives  83.9 us (25%)
  matrix products  82.4 us (25%)
  starting transfers between devices  7.86 us (2%)
  other arithmetic  7.53 us (2%)
  local copies, waits for them, and re-layouts  5.57 us (2%)
    all_to_all x2, waiting for transfers between devices, moe_layer(): lax.all_to_all(partial_value, 'expert', split_axis=0, concat_axis=0, tile...  134 us
    all_to_all x2, blocking collectives, moe_layer(): lax.all_to_all(copies, 'expert', split_axis=0, concat_axis=0, tiled=True)  83.9 us
    dot_general x2, matrix products, expert_rows(): output = jnp.dot(hidden, down_rows, preferred_element_type=jnp.float32)  28.2 us
    dot_general x2, matrix products, expert_rows(): up_value = jnp.dot(matrix, up_cols, preferred_element_type=jnp.float32)  25 us
    dot_general x2, matrix products, expert_rows(): gate_value = jnp.dot(matrix, gate_cols, preferred_element_type=jnp.float32)  24.8 us
    ppermute x2, waiting for transfers between devices, shifted(): return lax.ppermute(x, axis, [(i, (i + by) % size) for i in range(size)])  11.5 us
    all_to_all x2, starting transfers between devices, moe_layer(): lax.all_to_all(partial_value, 'expert', split_axis=0, concat_axis=0, tile...  7.56 us
  transfers between devices with their start and end apart: 4, of which 4 were waited for; matrix products, arithmetic and copies ran while one was open for 2% of the time, Pallas kernels for 0%

commit v1 on v0

v1 whole, which is shorter than its diff:
```python
import jax
import jax.numpy as jnp
from jax import lax
from jax.experimental import pallas as pl
from jax.experimental.pallas import tpu as pltpu
from jax.sharding import PartitionSpec as P


EXPERTS = 4
STEPS = 2
CAP = 24
SPAN = EXPERTS * CAP
EIGHTHS = (3, 3, 2)
MIB = 1 << 20
epsilon = 1e-05


HBM = pl.BlockSpec(memory_space=pl.ANY)
WHOLE = pl.BlockSpec(memory_space=pltpu.VMEM)


def in_hbm(w):
    return pltpu.with_memory_space_constraint(w, pltpu.HBM)


def in_vmem(w):
    return pltpu.with_memory_space_constraint(w, pltpu.VMEM)


def limit(n):
    return pltpu.CompilerParams(vmem_limit_bytes=int(n))


def tile_of(width, most):
    return next(t for t in (most, 256, 128, width) if width % t == 0)


def call(kernel, *args, keep=(), after=(), **kwargs):
    count, extra = len(args), len(keep) + len(after)
    body = lambda *refs: kernel(*refs[:count], *refs[count + extra:])
    specs = kwargs.pop("in_specs", [WHOLE] * count)
    return pl.pallas_call(body, in_specs=list(specs) + [WHOLE] * len(keep) + [HBM] * len(after), **kwargs)(*args, *map(in_vmem, keep), *after)


def own_expert():
    return lax.axis_index("expert") // (lax.axis_size("expert") // EXPERTS)


def slot_table(chosen, first, second):
    tokens = chosen.shape[0]
    own = own_expert()
    a, b = chosen[:, 0:1] ^ own, chosen[:, 1:2] ^ own
    lane = lax.broadcasted_iota(jnp.int32, (tokens, 128), 1)
    hit = ((a == lane) | (b == lane)).astype(jnp.float32)
    earlier = lax.broadcasted_iota(jnp.int32, (tokens, tokens), 1) < lax.broadcasted_iota(jnp.int32, (tokens, tokens), 0)
    before = jnp.dot(earlier.astype(jnp.float32), hit, preferred_element_type=jnp.float32).astype(jnp.int32)
    column = lax.broadcasted_iota(jnp.int32, (tokens, SPAN), 1)
    table = jnp.zeros((tokens, SPAN), jnp.float32)
    for k in range(EXPERTS):
        share = jnp.where(a == k, first, jnp.where(b == k, second, 0.0))
        table = jnp.where(column == k * CAP + before[:, k:k + 1], share, table)
    return table


def route_kernel(t, parts, arrives):
    def kernel(*refs):
        x_refs, refs = refs[:parts], refs[parts:]
        arriving_ref, refs = (refs[0], refs[1:]) if arrives else (None, refs)
        scale_ref, chosen_ref, normed_ref, *refs = refs
        x = jnp.concatenate([ref[...] for ref in x_refs], 1) if parts > 1 else x_refs[0][...]
        if arrives:
            piece_refs, x_ref = refs[:-1], refs[-1]
            x = jnp.where(lax.axis_index("section") == 0, arriving_ref[...], x)
            x_ref[...] = x
        else:
            piece_refs = refs
        x = x.astype(jnp.float32)
        mean = jnp.mean(x * x, -1, keepdims=True)
        normed = (x * lax.rsqrt(mean + epsilon) * scale_ref[...]).astype(jnp.bfloat16)
        normed_ref[...] = normed
        table = slot_table(chosen_ref[t], 1.0, 1.0).astype(jnp.bfloat16)
        rows = lax.dot_general(table, normed, (((0,), (0,)), ((), ())), preferred_element_type=jnp.float32).astype(jnp.bfloat16)
        for k, ref in enumerate(piece_refs):
            ref[...] = rows[k * CAP:(k + 1) * CAP]

    return kernel


def route(t, x_parts, arriving, scale, chosen):
    tokens, width = x_parts[0].shape[0], scale.shape[1]
    whole = jax.ShapeDtypeStruct((tokens, width), jnp.bfloat16)
    piece = jax.ShapeDtypeStruct((CAP, width), jnp.bfloat16)
    arrives = arriving is not None
    return call(
        route_kernel(t, len(x_parts), arrives),
        *x_parts, *([arriving] if arrives else []), scale, chosen,
        out_shape=[whole] + [piece] * EXPERTS + [whole] * arrives,
        compiler_params=limit(8 * MIB),
        name="route",
    )


def share_kernel(t):
    def kernel(normed_ref, router_ref, chosen_ref, table_ref):
        normed = normed_ref[...].astype(jnp.float32)
        chosen = chosen_ref[t]
        logits = [jnp.sum(normed * router_ref[e:e + 1, :], -1, keepdims=True) for e in range(EXPERTS)]
        picked = [sum(jnp.where(chosen[:, c:c + 1] == e, logits[e], 0.0) for e in range(EXPERTS)) for c in range(2)]
        first = jax.nn.sigmoid(picked[0] - picked[1])
        table_ref[...] = slot_table(chosen, first, 1.0 - first).astype(jnp.bfloat16)

    return kernel


def share_table(t, normed, router, chosen):
    return call(
        share_kernel(t),
        normed, router, chosen,
        out_shape=jax.ShapeDtypeStruct((normed.shape[0], SPAN), jnp.bfloat16),
        compiler_params=limit(4 * MIB),
        cost_estimate=pl.CostEstimate(flops=300_000_000, bytes_accessed=0, transcendentals=0),
        name="share_table",
    )


def fetch(w, rows, columns, after):
    def kernel(source_ref, target_ref):
        pltpu.sync_copy(source_ref.at[pl.ds(*rows), pl.ds(*columns)], target_ref)

    return call(
        kernel,
        in_hbm(w),
        after=after,
        in_specs=[HBM],
        out_specs=WHOLE,
        out_shape=pltpu.VMEM((rows[1], columns[1]), w.dtype),
        compiler_params=limit(MIB),
        cost_estimate=pl.CostEstimate(flops=300 * rows[1] * columns[1], bytes_accessed=4 * rows[1] * columns[1], transcendentals=0),
        name="fetch",
    )


def gather_kernel(*refs):
    *piece_refs, low_ref, high_ref = refs
    half = low_ref.shape[1]
    for i, ref in enumerate(piece_refs):
        low_ref[i * CAP:(i + 1) * CAP, :] = ref[:, :half]
        high_ref[i * CAP:(i + 1) * CAP, :] = ref[:, half:]


def gather(pieces):
    return call(
        gather_kernel,
        *pieces,
        out_shape=[jax.ShapeDtypeStruct((len(pieces) * CAP, pieces[0].shape[1] // 2), jnp.bfloat16)] * 2,
        compiler_params=limit(MIB),
        name="gather",
    )


def expand_kernel(low_ref, high_ref, held_ref, gate_ref, up_ref, hidden_ref, ring_ref, sems, gate_sum_ref, up_sum_ref):
    half = held_ref.shape[0]
    tile = ring_ref.shape[2]
    count = hidden_ref.shape[1] // tile
    streams = ((up_ref, 0), (up_ref, 1), (gate_ref, 1))

    def copy(n, j):
        ref, k = streams[j]
        source = ref.at[pl.ds(k * half, half), pl.ds(pl.multiple_of(n * tile, tile), tile)]
        return pltpu.make_async_copy(source, ring_ref.at[j], sems.at[j])

    for j in range(len(streams)):
        copy(0, j).start()

    def step(n, carry):
        def product(rows_ref, j):
            copy(n, j).wait()
            return jnp.dot(rows_ref[...], ring_ref[j], preferred_element_type=jnp.float32)

        def refill(j):
            @pl.when(n + 1 < count)
            def _():
                copy(n + 1, j).start()

        columns = pl.ds(pl.multiple_of(n * tile, tile), tile)
        gate_sum_ref[...] = jnp.dot(low_ref[...], held_ref[:, columns], preferred_element_type=jnp.float32)
        up_sum_ref[...] = product(low_ref, 0)
        refill(0)
        up_sum_ref[...] += product(high_ref, 1)
        refill(1)
        gate = gate_sum_ref[...] + product(high_ref, 2)
        refill(2)
        hidden_ref[:, columns] = (gate * jax.nn.sigmoid(gate) * up_sum_ref[...]).astype(jnp.bfloat16)
        return carry

    lax.fori_loop(0, count, step, 0)


def expand(low, high, held, gate_w, up_w):
    depth, units = up_w.shape
    tile = tile_of(units, 512)
    total = low.shape[0]
    half = held.shape[0]
    return call(
        expand_kernel,
        low, high, in_vmem(held), in_hbm(gate_w), in_hbm(up_w),
        in_specs=[WHOLE] * 3 + [HBM] * 2,
        out_shape=jax.ShapeDtypeStruct((total, units), jnp.bfloat16),
        scratch_shapes=[pltpu.VMEM((3, half, tile), jnp.bfloat16), pltpu.SemaphoreType.DMA((3,)), pltpu.VMEM((total, tile), jnp.float32), pltpu.VMEM((total, tile), jnp.float32)],
        compiler_params=limit(6 * half * tile + 12 * total * tile + 5 * total * half),
        cost_estimate=pl.CostEstimate(flops=4 * total * depth * units, bytes_accessed=2 * depth * units, transcendentals=total * units),
        name="expand",
    )


def contract_kernel(hidden_ref, down_ref, own_ref, *other):
    width = down_ref.shape[1]
    tile = tile_of(width, 512)
    for start in range(0, width, tile):
        columns = slice(start, start + tile)
        out = jnp.dot(hidden_ref[...], down_ref[:, columns], preferred_element_type=jnp.float32)
        own_ref[:, columns] = out[:SPAN]
        for m, ref in enumerate(other):
            ref[:, columns] = out[(m + 1) * SPAN:(m + 2) * SPAN].astype(jnp.bfloat16)


def contract(hidden, held, keep, after):
    total, units = hidden.shape
    width = held.shape[1]
    tile = tile_of(width, 512)
    others = total // SPAN - 1
    return call(
        contract_kernel,
        hidden, in_vmem(held),
        keep=keep,
        after=after,
        out_shape=[jax.ShapeDtypeStruct((SPAN, width), jnp.float32)] + [jax.ShapeDtypeStruct((SPAN, width), jnp.bfloat16)] * others,
        compiler_params=limit(16 * total * tile + 2 * MIB),
        cost_estimate=pl.CostEstimate(flops=2 * total * width * units, bytes_accessed=2 * width * units, transcendentals=0),
        name="contract",
    )


def merge_kernel(*refs):
    own_ref, other_refs, piece_refs = refs[0], refs[1:-EXPERTS], refs[-EXPERTS:]
    total = own_ref[...]
    for ref in other_refs:
        total = total + ref[...].astype(jnp.float32)
    total = total.astype(jnp.bfloat16)
    for k, ref in enumerate(piece_refs):
        ref[...] = total[k * CAP:(k + 1) * CAP]


def merge(own, others):
    return call(
        merge_kernel,
        own, *others,
        out_shape=[jax.ShapeDtypeStruct((CAP, own.shape[1]), jnp.bfloat16)] * EXPERTS,
        compiler_params=limit(4 * MIB),
        name="merge",
    )


def combine_kernel(start):
    def kernel(table_ref, x_ref, *refs):
        *piece_refs, out_ref = refs
        rows = jnp.concatenate([ref[...] for ref in piece_refs], 0)
        mixture = jnp.dot(table_ref[...], rows, preferred_element_type=jnp.float32)
        x = x_ref[:, start:start + out_ref.shape[1]].astype(jnp.float32)
        out_ref[...] = (x + mixture).astype(jnp.bfloat16)

    return kernel


def combine(table, x, pieces, start):
    return call(
        combine_kernel(start),
        table, x, *pieces,
        out_shape=jax.ShapeDtypeStruct((x.shape[0], pieces[0].shape[1]), jnp.bfloat16),
        compiler_params=limit(4 * MIB),
        name="combine",
    )


def over_experts(v, k):
    group = lax.axis_size("expert") // EXPERTS
    return lax.ppermute(v, "expert", [(e * group + j, (e ^ k) * group + j) for e in range(EXPERTS) for j in range(group)]) if k else v


def over_group(v, m):
    group = lax.axis_size("expert") // EXPERTS
    return lax.ppermute(v, "expert", [(e * group + j, e * group + (j + m) % group) for e in range(EXPERTS) for j in range(group)])


def over_sections(v):
    n = lax.axis_size("section")
    return lax.ppermute(v, "section", [(i, (i + 1) % n) for i in range(n)])


def moe_layer(t, x_parts, arriving, chosen, scale, router, gate_w, up_w, down_w, held):
    group = lax.axis_size("expert") // EXPERTS
    width = down_w.shape[1]
    normed, *routed = route(t, x_parts, arriving, scale, chosen)
    x = x_parts[0] if arriving is None else routed.pop()
    mine = [None] * EXPERTS
    for k in (3, 2, 1, 0):
        mine[k] = over_experts(routed[k], k)
    pieces = list(mine)
    for m in range(1, group):
        for piece in mine:
            pieces.append(over_group(piece, m))
    table = share_table(t, normed, router, chosen)
    widths = [width * e // 8 for e in EIGHTHS]
    starts = [sum(widths[:c]) for c in range(len(widths))]
    if not held:
        half = gate_w.shape[0] // 2
        down = []
        for span in zip(starts, widths):
            down.append(fetch(down_w, (0, down_w.shape[0]), span, [routed[0]]))
        gate = fetch(gate_w, (0, half), (0, gate_w.shape[1]), [routed[0]])
        held = gate, *down
    hidden = expand(*gather(pieces), held[0], gate_w, up_w)
    outs = []
    after = []
    for c, start in enumerate(starts):
        own, *others = contract(hidden, held[1 + c], [h for i, h in enumerate(held) if i != 1 + c], after)
        after = [own]
        others = [over_group(other, -m) for m, other in enumerate(others, 1)]
        back = list(merge(own, others))
        for k in (3, 2, 1):
            back[k] = over_experts(back[k], k)
        out = combine(table, x, back, start)
        outs.append(over_sections(out))
    return outs, held


def shards(pending, arriving, assignment, scale, router, gate_w, up_w, down_w):
    chosen = assignment[0]
    columns = router[0].T
    parts = [pending[0]]
    records = []
    held = ()
    for t in range(STEPS):
        parts, held = moe_layer(t, parts, arriving[t - 1] if t else None, chosen, scale, columns, gate_w[0], up_w[0], down_w[0], held)
        records.append(jnp.concatenate(parts, -1))
    return jnp.stack(records)[:, None]


def solution(mesh):
    return jax.shard_map(
        shards,
        mesh=mesh,
        in_specs=(
            P("section", "expert", None),
            P(None, "expert", None),
            P("section", None, "expert", None),
            P("section", None),
            P("section", None, None),
            P("section", None, "expert"),
            P("section", None, "expert"),
            P("section", "expert", None),
        ),
        out_specs=P(None, "section", "expert", None),
        check_vma=False,
    )
```

time: 334 us -> 198 us (0.59)
  waiting for transfers between devices: 146 us -> 48.7 us
  blocking collectives: 83.9 us -> 0 us
  matrix products: 82.4 us -> 0 us
  Pallas kernels: 0 us -> 78.7 us
  starting transfers between devices: 7.86 us -> 58.4 us
  other arithmetic: 7.53 us -> 0.88 us
  local copies, waits for them, and re-layouts: 5.57 us -> 10.7 us
    all_to_all x2 -> x0, waiting for transfers between devices: 134 us -> none  [moe_layer(): lax.all_to_all(partial_value, 'expert', split_axis=0, concat_axis=0, tile...]
    all_to_all x2 -> x0, blocking collectives: 83.9 us -> none  [moe_layer(): lax.all_to_all(copies, 'expert', split_axis=0, concat_axis=0, tiled=True)]
    dot_general x12 -> x0, matrix products: 82.4 us -> none  [the longest x2 28.2 us: expert_rows(): output = jnp.dot(hidden, down_rows, preferred_element_type=jnp.float32)]
    pallas_call x0 -> x30, Pallas kernels: none -> 78.7 us  [call(): pl.pallas_call(body, in_specs=list(specs) + [WHOLE] * len(keep) + [HBM] *...]
    ppermute x2 -> x44, starting transfers between devices: 0.3 us -> 58.4 us  [the longest x24 43 us: over_experts(): lax.ppermute(v, 'expert', [(e * group + j, (e ^ k) * group + j) for e in...]
    ppermute x2 -> x44, waiting for transfers between devices: 11.5 us -> 48.7 us  [the longest x14 21.4 us: over_group(): lax.ppermute(v, 'expert', [(e * group + j, e * group + (j + m) % group) f...]
    unnamed x22 -> x36, local copies, waits for them, and re-layouts: 0.74 us -> 9.92 us
    all_to_all x2 -> x0, starting transfers between devices: 7.56 us -> none  [moe_layer(): lax.all_to_all(partial_value, 'expert', split_axis=0, concat_axis=0, tile...]
  transfers between devices with their start and end apart: 4 -> 44, of which waited for: 4 -> 20; matrix products, arithmetic and copies ran while one was open for 2% -> 0% of each run, Pallas kernels for 0% -> 17%
where the time goes in v1:
time: 198 us
  Pallas kernels  78.7 us (40%)
  starting transfers between devices  58.4 us (29%)
  waiting for transfers between devices  48.7 us (25%)
  local copies, waits for them, and re-layouts  10.7 us (5%)
    pallas_call x30, Pallas kernels, call(): pl.pallas_call(body, in_specs=list(specs) + [WHOLE] * len(keep) + [HBM] *...  78.7 us
    ppermute x24, starting transfers between devices, over_experts(): lax.ppermute(v, 'expert', [(e * group + j, (e ^ k) * group + j) for e in...  43 us
    ppermute x14, waiting for transfers between devices, over_group(): lax.ppermute(v, 'expert', [(e * group + j, e * group + (j + m) % group) f...  21.4 us
    ppermute x24, waiting for transfers between devices, over_experts(): lax.ppermute(v, 'expert', [(e * group + j, (e ^ k) * group + j) for e in...  19.6 us
    ppermute x14, starting transfers between devices, over_group(): lax.ppermute(v, 'expert', [(e * group + j, e * group + (j + m) % group) f...  12.7 us
    unnamed x36, local copies, waits for them, and re-layouts  9.92 us
    ppermute x6, waiting for transfers between devices, over_sections(): return lax.ppermute(v, 'section', [(i, (i + 1) % n) for i in range(n)])  7.68 us
  transfers between devices with their start and end apart: 44, of which 20 were waited for; matrix products, arithmetic and copies ran while one was open for 0% of the time, Pallas kernels for 17%

profile of v1, /device:TPU:0, one launch (start us, length us, event | category | flops | bytes accessed | tf_op | source)
XLA Modules:
  0.0 197.8 jit_solution(4857357649692443319)
XLA Ops:
  0.0 0.8 copy.9.refs_2_.refs_5_
  0.8 0.9 copy-done.4
  1.7 0.7 copy-done.7
  2.4 0.7 route.2
  3.1 3.1 %collective-permute-start = (bf16[24,4096]{1,0:T(8,128)(2,1)S(1)}, bf16[24,4096]{1,0:T(8,128)(2,1)S(1)}, u32[]{:S(2)}, u32[]{:S(2)}) collective-permute-start(bf16[24,4096]{1,0:T(8,128)(2,1)S(1)} %get-tuple-element.58), channel_id=1, source_target_pairs={{0,2},{1,3},{2,0},{3,1},{4,6},{5,7},{6,4},{7,5},{8,10},{9,11},{10,... | collective-permute-start | bytes 589832 | tf_op jit(solution)/shard_map/ppermute | solution.py:287
  6.3 2.6 %collective-permute-start.1 = (bf16[24,4096]{1,0:T(8,128)(2,1)S(1)}, bf16[24,4096]{1,0:T(8,128)(2,1)S(1)}, u32[]{:S(2)}, u32[]{:S(2)}) collective-permute-start(bf16[24,4096]{1,0:T(8,128)(2,1)S(1)} %get-tuple-element.59), channel_id=1, source_target_pairs={{0,4},{1,5},{2,6},{3,7},{4,0},{5,1},{6,2},{7,3},{8,12},{9,13},{10,... | collective-permute-start | bytes 589832 | tf_op jit(solution)/shard_map/ppermute | solution.py:287
  8.8 1.7 collective-permute-start.3
  10.5 4.1 %fetch.6.refs_3_.refs_1_.refs_4_ = bf16[3584,1536]{1,0:T(8,128)(2,1)S(1)} custom-call(bf16[3584,4096]{1,0:T(8,128)(2,1)} %bitcast.30, bf16[24,4096]{1,0:T(8,128)(2,1)S(1)} %get-tuple-element.57.refs_0_.refs_1_), custom_call_target="tpu_custom_call" | custom-call | flops 1651507200 | bytes 22020096 | tf_op jit(solution)/shard_map/fetch/pallas_call | solution.py:42
  14.7 7.1 %fetch.7.refs_4_.refs_1_ = bf16[3584,1024]{1,0:T(8,128)(2,1)S(1)} custom-call(bf16[3584,4096]{1,0:T(8,128)(2,1)} %bitcast.31, bf16[24,4096]{1,0:T(8,128)(2,1)S(1)} %get-tuple-element.57.refs_0_.refs_1_), custom_call_target="tpu_custom_call" | custom-call | flops 1101004800 | bytes 14680064 | tf_op jit(solution)/shard_map/fetch/pallas_call | solution.py:42
  21.7 6.8 %fetch.5.refs_1_.refs_3_ = bf16[3584,1536]{1,0:T(8,128)(2,1)S(1)} custom-call(bf16[3584,4096]{1,0:T(8,128)(2,1)} %bitcast.32, bf16[24,4096]{1,0:T(8,128)(2,1)S(1)} %get-tuple-element.57.refs_0_.refs_1_), custom_call_target="tpu_custom_call" | custom-call | flops 1651507200 | bytes 22020096 | tf_op jit(solution)/shard_map/fetch/pallas_call | solution.py:42
  28.5 4.1 %copy-done.1 = bf16[3584,1536]{1,0:T(8,128)(2,1)} copy-done((bf16[3584,1536]{1,0:T(8,128)(2,1)}, bf16[3584,1536]{1,0:T(8,128)(2,1)S(1)}, u32[]{:S(2)}) %copy-start.1) | copy-done | bytes 11010072
  32.9 1.7 collective-permute-start.5
  34.9 5.2 %fetch.4.refs_2_ = bf16[2048,3584]{1,0:T(8,128)(2,1)S(1)} custom-call(bf16[4096,3584]{1,0:T(8,128)(2,1)} %bitcast.33, bf16[24,4096]{1,0:T(8,128)(2,1)S(1)} %get-tuple-element.57.refs_0_.refs_1_), custom_call_target="tpu_custom_call" | custom-call | flops 2202009600 | bytes 29360128 | tf_op jit(solution)/shard_map/fetch/pallas_call | solution.py:42
  40.4 4.1 %collective-permute-done.5.refs_6_ = bf16[24,4096]{1,0:T(8,128)(2,1)S(1)} collective-permute-done((bf16[24,4096]{1,0:T(8,128)(2,1)S(1)}, bf16[24,4096]{1,0:T(8,128)(2,1)S(1)}, u32[]{:S(2)}, u32[]{:S(2)}) %collective-permute-start.5) | collective-permute-done | bytes 196640 | tf_op jit(solution)/shard_map/ppermute | solution.py:292
  44.5 2.1 %collective-permute-done.6.refs_7_ = bf16[24,4096]{1,0:T(8,128)(2,1)S(1)} collective-permute-done((bf16[24,4096]{1,0:T(8,128)(2,1)S(1)}, bf16[24,4096]{1,0:T(8,128)(2,1)S(1)}, u32[]{:S(2)}, u32[]{:S(2)}) %collective-permute-start.6) | collective-permute-done | bytes 196640 | tf_op jit(solution)/shard_map/ppermute | solution.py:292
  46.7 17.1 %expand.2.refs_0_ = bf16[192,3584]{1,0:T(8,128)(2,1)S(1)} custom-call(bf16[192,2048]{1,0:T(8,128)(2,1)S(1)} %get-tuple-element.61.refs_0_, bf16[192,2048]{1,0:T(8,128)(2,1)S(1)} %get-tuple-element.62.refs_1_, bf16[2048,3584]{1,0:T(8,128)(2,1)S(1)} %fetch.4.refs_2_, bf16[4096,3584]{1,0:T(8,128)(2,1)} %bitcast.34, bf16[4096,3584]{1,0:T(8,128)(2,1)} %bitcast.36), custom_call_target="tpu_custom_call" | custom-call | flops 11274289152 | bytes 29360128 | tf_op jit(solution)/shard_map/expand/pallas_call | solution.py:42
  63.8 4.1 %copy-done.2 = bf16[3584,1536]{1,0:T(8,128)(2,1)S(1)} copy-done((bf16[3584,1536]{1,0:T(8,128)(2,1)S(1)}, bf16[3584,1536]{1,0:T(8,128)(2,1)}, u32[]{:S(2)}) %copy-start.2) | copy-done | bytes 11010072
  67.9 2.3 %contract.6 = (f32[96,1536]{1,0:T(8,128)S(1)}, bf16[96,1536]{1,0:T(8,128)(2,1)S(1)}) custom-call(bf16[192,3584]{1,0:T(8,128)(2,1)S(1)} %expand.2.refs_0_, bf16[3584,1536]{1,0:T(8,128)(2,1)S(1)} %copy-done.2, bf16[2048,3584]{1,0:T(8,128)(2,1)S(1)} %fetch.4.refs_2_, bf16[3584,1536]{1,0:T(8,128)(2,1)S(1)} %fetch.6.refs_3_.refs_1_.refs_4_, ...), custom_call_target="tpu_custom_call" | custom-call | flops 2113929216 | bytes 11010048 | tf_op jit(solution)/shard_map/contract/pallas_call | solution.py:42
  70.8 2.3 %contract.7 = (f32[96,1536]{1,0:T(8,128)S(1)}, bf16[96,1536]{1,0:T(8,128)(2,1)S(1)}) custom-call(bf16[192,3584]{1,0:T(8,128)(2,1)S(1)} %expand.2.refs_0_, bf16[3584,1536]{1,0:T(8,128)(2,1)S(1)} %fetch.6.refs_3_.refs_1_.refs_4_, bf16[2048,3584]{1,0:T(8,128)(2,1)S(1)} %fetch.4.refs_2_, bf16[3584,1536]{1,0:T(8,128)(2,1)S(1)} %copy-done.2, ...), custom_call_target="tpu_custom_call" | custom-call | flops 2113929216 | bytes 11010048 | tf_op jit(solution)/shard_map/contract/pallas_call | solution.py:42
  73.1 1.6 collective-permute-start.12
  74.7 1.6 contract.8
  76.9 3.2 %collective-permute-done.7.refs_1_ = bf16[96,1536]{1,0:T(8,128)(2,1)S(1)} collective-permute-done((bf16[96,1536]{1,0:T(8,128)(2,1)S(1)}, bf16[96,1536]{1,0:T(8,128)(2,1)S(1)}, u32[]{:S(2)}, u32[]{:S(2)}) %collective-permute-start.7) | collective-permute-done | bytes 294944 | tf_op jit(solution)/shard_map/ppermute | solution.py:292
  80.2 0.7 collective-permute-start.8
  80.9 3.5 %collective-permute-start.9 = (bf16[24,1536]{1,0:T(8,128)(2,1)S(1)}, bf16[24,1536]{1,0:T(8,128)(2,1)S(1)}, u32[]{:S(2)}, u32[]{:S(2)}) collective-permute-start(bf16[24,1536]{1,0:T(8,128)(2,1)S(1)} %get-tuple-element.67), channel_id=1, source_target_pairs={{0,4},{1,5},{2,6},{3,7},{4,0},{5,1},{6,2},{7,3},{8,12},{9,13},{10,... | collective-permute-start | bytes 221192 | tf_op jit(solution)/shard_map/ppermute | solution.py:287
  84.7 0.9 collective-permute-done.12.refs_1_
  85.6 0.6 collective-permute-start.13
  86.2 1.4 collective-permute-done.17.refs_1_
  87.6 2.0 %collective-permute-start.14 = (bf16[24,1536]{1,0:T(8,128)(2,1)S(1)}, bf16[24,1536]{1,0:T(8,128)(2,1)S(1)}, u32[]{:S(2)}, u32[]{:S(2)}) collective-permute-start(bf16[24,1536]{1,0:T(8,128)(2,1)S(1)} %get-tuple-element.73), channel_id=1, source_target_pairs={{0,4},{1,5},{2,6},{3,7},{4,0},{5,1},{6,2},{7,3},{8,12},{9,13},{10,... | collective-permute-start | bytes 221192 | tf_op jit(solution)/shard_map/ppermute | solution.py:287
  89.7 1.4 collective-permute-start.15
  91.2 0.6 collective-permute-start.18
  91.8 2.4 %collective-permute-start.19 = (bf16[24,1024]{1,0:T(8,128)(2,1)S(1)}, bf16[24,1024]{1,0:T(8,128)(2,1)S(1)}, u32[]{:S(2)}, u32[]{:S(2)}) collective-permute-start(bf16[24,1024]{1,0:T(8,128)(2,1)S(1)} %get-tuple-element.79), channel_id=1, source_target_pairs={{0,4},{1,5},{2,6},{3,7},{4,0},{5,1},{6,2},{7,3},{8,12},{9,13},{10,... | collective-permute-start | bytes 147464 | tf_op jit(solution)/shard_map/ppermute | solution.py:287
  94.2 1.4 collective-permute-start.20
  96.6 1.7 collective-permute-start.16
  98.6 1.5 collective-permute-done.20.refs_5_
  100.5 3.7 %collective-permute-done.21.refs_2_ = bf16[32,1024]{1,0:T(8,128)(2,1)S(1)} collective-permute-done((bf16[32,1024]{1,0:T(8,128)(2,1)S(1)}, bf16[32,1024]{1,0:T(8,128)(2,1)S(1)}, u32[]{:S(2)}, u32[]{:S(2)}) %collective-permute-start.21) | collective-permute-done | bytes 65568 | tf_op jit(solution)/shard_map/ppermute | solution.py:297
  104.2 0.7 route.3
  105.0 2.1 %collective-permute-start.23 = (bf16[24,4096]{1,0:T(8,128)(2,1)S(1)}, bf16[24,4096]{1,0:T(8,128)(2,1)S(1)}, u32[]{:S(2)}, u32[]{:S(2)}) collective-permute-start(bf16[24,4096]{1,0:T(8,128)(2,1)S(1)} %get-tuple-element.85), channel_id=1, source_target_pairs={{0,4},{1,5},{2,6},{3,7},{4,0},{5,1},{6,2},{7,3},{8,12},{9,13},{10,... | collective-permute-start | bytes 589832 | tf_op jit(solution)/shard_map/ppermute | solution.py:287
  107.0 2.3 %collective-permute-start.24 = (bf16[24,4096]{1,0:T(8,128)(2,1)S(1)}, bf16[24,4096]{1,0:T(8,128)(2,1)S(1)}, u32[]{:S(2)}, u32[]{:S(2)}) collective-permute-start(bf16[24,4096]{1,0:T(8,128)(2,1)S(1)} %get-tuple-element.86), channel_id=1, source_target_pairs={{0,6},{1,7},{2,4},{3,5},{4,2},{5,3},{6,0},{7,1},{8,14},{9,15},{10,... | collective-permute-start | bytes 589832 | tf_op jit(solution)/shard_map/ppermute | solution.py:287
  109.9 4.4 %collective-permute-done.22.refs_1_ = bf16[24,4096]{1,0:T(8,128)(2,1)S(1)} collective-permute-done((bf16[24,4096]{1,0:T(8,128)(2,1)S(1)}, bf16[24,4096]{1,0:T(8,128)(2,1)S(1)}, u32[]{:S(2)}, u32[]{:S(2)}) %collective-permute-start.22) | collective-permute-done | bytes 196640 | tf_op jit(solution)/shard_map/ppermute | solution.py:287
  114.8 7.3 %collective-permute-done.23.refs_2_ = bf16[24,4096]{1,0:T(8,128)(2,1)S(1)} collective-permute-done((bf16[24,4096]{1,0:T(8,128)(2,1)S(1)}, bf16[24,4096]{1,0:T(8,128)(2,1)S(1)}, u32[]{:S(2)}, u32[]{:S(2)}) %collective-permute-start.23) | collective-permute-done | bytes 196640 | tf_op jit(solution)/shard_map/ppermute | solution.py:287
  122.7 1.5 collective-permute-start.28
  124.2 3.6 %collective-permute-done.27.refs_6_ = bf16[24,4096]{1,0:T(8,128)(2,1)S(1)} collective-permute-done((bf16[24,4096]{1,0:T(8,128)(2,1)S(1)}, bf16[24,4096]{1,0:T(8,128)(2,1)S(1)}, u32[]{:S(2)}, u32[]{:S(2)}) %collective-permute-start.27) | collective-permute-done | bytes 196640 | tf_op jit(solution)/shard_map/ppermute | solution.py:292
  127.8 2.1 %collective-permute-done.28.refs_7_ = bf16[24,4096]{1,0:T(8,128)(2,1)S(1)} collective-permute-done((bf16[24,4096]{1,0:T(8,128)(2,1)S(1)}, bf16[24,4096]{1,0:T(8,128)(2,1)S(1)}, u32[]{:S(2)}, u32[]{:S(2)}) %collective-permute-start.28) | collective-permute-done | bytes 196640 | tf_op jit(solution)/shard_map/ppermute | solution.py:292
  130.1 22.2 %expand.3.refs_0_ = bf16[192,3584]{1,0:T(8,128)(2,1)S(1)} custom-call(bf16[192,2048]{1,0:T(8,128)(2,1)S(1)} %get-tuple-element.87.refs_0_, bf16[192,2048]{1,0:T(8,128)(2,1)S(1)} %get-tuple-element.88.refs_1_, bf16[2048,3584]{1,0:T(8,128)(2,1)S(1)} %fetch.4.refs_2_, bf16[4096,3584]{1,0:T(8,128)(2,1)} %bitcast.35, bf16[4096,3584]{1,0:T(8,128)(2,1)} %bitcast.37), custom_call_target="tpu_custom_call" | custom-call | flops 11274289152 | bytes 29360128 | tf_op jit(solution)/shard_map/expand/pallas_call | solution.py:42
  152.4 2.3 %contract.9 = (f32[96,1536]{1,0:T(8,128)S(1)}, bf16[96,1536]{1,0:T(8,128)(2,1)S(1)}) custom-call(bf16[192,3584]{1,0:T(8,128)(2,1)S(1)} %expand.3.refs_0_, bf16[3584,1536]{1,0:T(8,128)(2,1)S(1)} %bitcast.20, bf16[2048,3584]{1,0:T(8,128)(2,1)S(1)} %fetch.4.refs_2_, bf16[3584,1536]{1,0:T(8,128)(2,1)S(1)} %bitcast.18, bf16[3584,1024]{1,0:T(8,128)(2,1)S(1)} %bitcast.22), custom_call_target="tpu_custom_call" | custom-call | flops 2113929216 | bytes 11010048 | tf_op jit(solution)/shard_map/contract/pallas_call | solution.py:42
  155.3 2.3 %contract.10 = (f32[96,1536]{1,0:T(8,128)S(1)}, bf16[96,1536]{1,0:T(8,128)(2,1)S(1)}) custom-call(bf16[192,3584]{1,0:T(8,128)(2,1)S(1)} %expand.3.refs_0_, bf16[3584,1536]{1,0:T(8,128)(2,1)S(1)} %bitcast.18, bf16[2048,3584]{1,0:T(8,128)(2,1)S(1)} %fetch.4.refs_2_, bf16[3584,1536]{1,0:T(8,128)(2,1)S(1)} %bitcast.20, bf16[3584,1024]{1,0:T(8,128)(2,1)S(1)} %bitcast.22, ...), custom_call_target="tpu_custom_call" | custom-call | flops 2113929216 | bytes 11010048 | tf_op jit(solution)/shard_map/contract/pallas_call | solution.py:42
  157.6 1.6 collective-permute-start.34
  159.2 1.6 contract.11
  160.8 0.6 collective-permute-start.39
  161.4 1.7 collective-permute-done.29.refs_1_
  163.1 3.3 %collective-permute-start.30 = (bf16[24,1536]{1,0:T(8,128)(2,1)S(1)}, bf16[24,1536]{1,0:T(8,128)(2,1)S(1)}, u32[]{:S(2)}, u32[]{:S(2)}) collective-permute-start(bf16[24,1536]{1,0:T(8,128)(2,1)S(1)} %get-tuple-element.92), channel_id=1, source_target_pairs={{0,2},{1,3},{2,0},{3,1},{4,6},{5,7},{6,4},{7,5},{8,10},{9,11},{10,... | collective-permute-start | bytes 221192 | tf_op jit(solution)/shard_map/ppermute | solution.py:287
  166.4 1.9 collective-permute-done.39.refs_1_
  168.4 6.2 %collective-permute-start.40 = (bf16[24,1024]{1,0:T(8,128)(2,1)S(1)}, bf16[24,1024]{1,0:T(8,128)(2,1)S(1)}, u32[]{:S(2)}, u32[]{:S(2)}) collective-permute-start(bf16[24,1024]{1,0:T(8,128)(2,1)S(1)} %get-tuple-element.104), channel_id=1, source_target_pairs={{0,2},{1,3},{2,0},{3,1},{4,6},{5,7},{6,4},{7,5},{8,10},{9,11},{10,... | collective-permute-start | bytes 147464 | tf_op jit(solution)/shard_map/ppermute | solution.py:287
  174.6 2.4 %collective-permute-start.42 = (bf16[24,1024]{1,0:T(8,128)(2,1)S(1)}, bf16[24,1024]{1,0:T(8,128)(2,1)S(1)}, u32[]{:S(2)}, u32[]{:S(2)}) collective-permute-start(bf16[24,1024]{1,0:T(8,128)(2,1)S(1)} %get-tuple-element.106), channel_id=1, source_target_pairs={{0,6},{1,7},{2,4},{3,5},{4,2},{5,3},{6,0},{7,1},{8,14},{9,15},{10,... | collective-permute-start | bytes 147464 | tf_op jit(solution)/shard_map/ppermute | solution.py:287
  177.6 3.0 %collective-permute-start.32 = (bf16[24,1536]{1,0:T(8,128)(2,1)S(1)}, bf16[24,1536]{1,0:T(8,128)(2,1)S(1)}, u32[]{:S(2)}, u32[]{:S(2)}) collective-permute-start(bf16[24,1536]{1,0:T(8,128)(2,1)S(1)} %get-tuple-element.94), channel_id=1, source_target_pairs={{0,6},{1,7},{2,4},{3,5},{4,2},{5,3},{6,0},{7,1},{8,14},{9,15},{10,... | collective-permute-start | bytes 221192 | tf_op jit(solution)/shard_map/ppermute | solution.py:287
  180.6 4.4 %collective-permute-done.41.refs_4_ = bf16[24,1024]{1,0:T(8,128)(2,1)S(1)} collective-permute-done((bf16[24,1024]{1,0:T(8,128)(2,1)S(1)}, bf16[24,1024]{1,0:T(8,128)(2,1)S(1)}, u32[]{:S(2)}, u32[]{:S(2)}) %collective-permute-start.41) | collective-permute-done | bytes 49184 | tf_op jit(solution)/shard_map/ppermute | solution.py:287
  184.9 1.6 collective-permute-start.36
  186.5 2.8 %collective-permute-start.37 = (bf16[24,1536]{1,0:T(8,128)(2,1)S(1)}, bf16[24,1536]{1,0:T(8,128)(2,1)S(1)}, u32[]{:S(2)}, u32[]{:S(2)}) collective-permute-start(bf16[24,1536]{1,0:T(8,128)(2,1)S(1)} %get-tuple-element.100), channel_id=1, source_target_pairs={{0,6},{1,7},{2,4},{3,5},{4,2},{5,3},{6,0},{7,1},{8,14},{9,15},{10,... | collective-permute-start | bytes 221192 | tf_op jit(solution)/shard_map/ppermute | solution.py:287
  190.3 0.6 collective-permute-start.33
  190.9 1.7 collective-permute-done.37.refs_5_
  192.9 0.8 collective-permute-done.43
  193.8 1.1 collective-permute-done.33
  194.8 2.1 %collective-permute-done.38 = bf16[32,1536]{1,0:T(8,128)(2,1)S(1)} collective-permute-done((bf16[32,1536]{1,0:T(8,128)(2,1)S(1)}, bf16[32,1536]{1,0:T(8,128)(2,1)S(1)}, u32[]{:S(2)}, u32[]{:S(2)}) %collective-permute-start.38) | collective-permute-done | bytes 98336 | tf_op jit(solution)/shard_map/ppermute | solution.py:297
  197.0 0.8 maximum_bitcast_fusion
  (97 shorter events, 8.6 us)
Async XLA Ops:
  0.8 1.0 copy-start.4
  1.7 0.7 copy-start.7
  3.1 29.5 %collective-permute-start = (bf16[24,4096]{1,0:T(8,128)(2,1)S(1)}, bf16[24,4096]{1,0:T(8,128)(2,1)S(1)}, u32[]{:S(2)}, u32[]{:S(2)}) collective-permute-start(bf16[24,4096]{1,0:T(8,128)(2,1)S(1)} %get-tuple-element.58), channel_id=1, source_target_pairs={{0,2},{1,3},{2,0},{3,1},{4,6},{5,7},{6,4},{7,5},{8,10},{9,11},{10,... | collective-permute-start | bytes 589832 | tf_op jit(solution)/shard_map/ppermute | solution.py:287
  6.3 26.7 %collective-permute-start.1 = (bf16[24,4096]{1,0:T(8,128)(2,1)S(1)}, bf16[24,4096]{1,0:T(8,128)(2,1)S(1)}, u32[]{:S(2)}, u32[]{:S(2)}) collective-permute-start(bf16[24,4096]{1,0:T(8,128)(2,1)S(1)} %get-tuple-element.59), channel_id=1, source_target_pairs={{0,4},{1,5},{2,6},{3,7},{4,0},{5,1},{6,2},{7,3},{8,12},{9,13},{10,... | collective-permute-start | bytes 589832 | tf_op jit(solution)/shard_map/ppermute | solution.py:287
  8.8 25.8 %collective-permute-start.2 = (bf16[24,4096]{1,0:T(8,128)(2,1)S(1)}, bf16[24,4096]{1,0:T(8,128)(2,1)S(1)}, u32[]{:S(2)}, u32[]{:S(2)}) collective-permute-start(bf16[24,4096]{1,0:T(8,128)(2,1)S(1)} %get-tuple-element.60), channel_id=1, source_target_pairs={{0,6},{1,7},{2,4},{3,5},{4,2},{5,3},{6,0},{7,1},{8,14},{9,15},{10,... | collective-permute-start | bytes 589832 | tf_op jit(solution)/shard_map/ppermute | solution.py:287
  8.8 31.3 %collective-permute-start.3 = (bf16[24,4096]{1,0:T(8,128)(2,1)S(1)}, bf16[24,4096]{1,0:T(8,128)(2,1)S(1)}, u32[]{:S(2)}, u32[]{:S(2)}) collective-permute-start(bf16[24,4096]{1,0:T(8,128)(2,1)S(1)} %get-tuple-element.57.refs_0_.refs_1_), channel_id=1, source_target_pairs={{0,1},{1,0},{2,3},{3,2},{4,5},{5,4},{6,7},{7,6},{8,9},{9,8},{10,11... | collective-permute-start | bytes 589832 | tf_op jit(solution)/shard_map/ppermute | solution.py:292
  14.7 60.0 %copy-start = (bf16[3584,1536]{1,0:T(8,128)(2,1)}, bf16[3584,1536]{1,0:T(8,128)(2,1)S(1)}, u32[]{:S(2)}) copy-start(bf16[3584,1536]{1,0:T(8,128)(2,1)S(1)} %fetch.6.refs_3_.refs_1_.refs_4_) | copy-start | bytes 33030148
  21.7 52.9 %copy-start.3 = (bf16[3584,1024]{1,0:T(8,128)(2,1)}, bf16[3584,1024]{1,0:T(8,128)(2,1)S(1)}, u32[]{:S(2)}) copy-start(bf16[3584,1024]{1,0:T(8,128)(2,1)S(1)} %fetch.7.refs_4_.refs_1_) | copy-start | bytes 22020100
  28.5 4.1 %copy-start.1 = (bf16[3584,1536]{1,0:T(8,128)(2,1)}, bf16[3584,1536]{1,0:T(8,128)(2,1)S(1)}, u32[]{:S(2)}) copy-start(bf16[3584,1536]{1,0:T(8,128)(2,1)S(1)} %fetch.5.refs_1_.refs_3_) | copy-start | bytes 33030148
  32.6 7.8 %collective-permute-start.4 = (bf16[24,4096]{1,0:T(8,128)(2,1)S(1)}, bf16[24,4096]{1,0:T(8,128)(2,1)S(1)}, u32[]{:S(2)}, u32[]{:S(2)}) collective-permute-start(bf16[24,4096]{1,0:T(8,128)(2,1)S(1)} %collective-permute-done.refs_1_), channel_id=1, source_target_pairs={{0,1},{1,0},{2,3},{3,2},{4,5},{5,4},{6,7},{7,6},{8,9},{9,8},{10,11... | collective-permute-start | bytes 589832 | tf_op jit(solution)/shard_map/ppermute | solution.py:292
  32.9 11.6 %collective-permute-start.5 = (bf16[24,4096]{1,0:T(8,128)(2,1)S(1)}, bf16[24,4096]{1,0:T(8,128)(2,1)S(1)}, u32[]{:S(2)}, u32[]{:S(2)}) collective-permute-start(bf16[24,4096]{1,0:T(8,128)(2,1)S(1)} %collective-permute-done.1.refs_2_), channel_id=1, source_target_pairs={{0,1},{1,0},{2,3},{3,2},{4,5},{5,4},{6,7},{7,6},{8,9},{9,8},{10,11... | collective-permute-start | bytes 589832 | tf_op jit(solution)/shard_map/ppermute | solution.py:292
  34.6 12.0 %collective-permute-start.6 = (bf16[24,4096]{1,0:T(8,128)(2,1)S(1)}, bf16[24,4096]{1,0:T(8,128)(2,1)S(1)}, u32[]{:S(2)}, u32[]{:S(2)}) collective-permute-start(bf16[24,4096]{1,0:T(8,128)(2,1)S(1)} %collective-permute-done.2.refs_3_), channel_id=1, source_target_pairs={{0,1},{1,0},{2,3},{3,2},{4,5},{5,4},{6,7},{7,6},{8,9},{9,8},{10,11... | collective-permute-start | bytes 589832 | tf_op jit(solution)/shard_map/ppermute | solution.py:292
  63.8 4.1 %copy-start.2 = (bf16[3584,1536]{1,0:T(8,128)(2,1)S(1)}, bf16[3584,1536]{1,0:T(8,128)(2,1)}, u32[]{:S(2)}) copy-start(bf16[3584,1536]{1,0:T(8,128)(2,1)} %copy-done.1) | copy-start | bytes 33030148
  70.2 9.9 %collective-permute-start.7 = (bf16[96,1536]{1,0:T(8,128)(2,1)S(1)}, bf16[96,1536]{1,0:T(8,128)(2,1)S(1)}, u32[]{:S(2)}, u32[]{:S(2)}) collective-permute-start(bf16[96,1536]{1,0:T(8,128)(2,1)S(1)} %get-tuple-element.64), channel_id=1, source_target_pairs={{0,1},{1,0},{2,3},{3,2},{4,5},{5,4},{6,7},{7,6},{8,9},{9,8},{10,11... | collective-permute-start | bytes 884744 | tf_op jit(solution)/shard_map/ppermute | solution.py:292
  73.1 12.4 %collective-permute-start.12 = (bf16[96,1536]{1,0:T(8,128)(2,1)S(1)}, bf16[96,1536]{1,0:T(8,128)(2,1)S(1)}, u32[]{:S(2)}, u32[]{:S(2)}) collective-permute-start(bf16[96,1536]{1,0:T(8,128)(2,1)S(1)} %get-tuple-element.70), channel_id=1, source_target_pairs={{0,1},{1,0},{2,3},{3,2},{4,5},{5,4},{6,7},{7,6},{8,9},{9,8},{10,11... | collective-permute-start | bytes 884744 | tf_op jit(solution)/shard_map/ppermute | solution.py:292
  74.7 21.0 %copy-start.9 = (f32[1,4096,4]{1,2,0:T(4,128)S(1)}, f32[1,4096,4]{1,2,0:T(4,128)}, u32[]{:S(2)}) copy-start(f32[1,4096,4]{1,2,0:T(4,128)} %param.12) | copy-start | bytes 196612
  74.7 21.5 %copy-start.5 = (bf16[1,32,4096]{2,1,0:T(8,128)(2,1)S(1)}, bf16[1,32,4096]{2,1,0:T(8,128)(2,1)}, u32[]{:S(2)}) copy-start(bf16[1,32,4096]{2,1,0:T(8,128)(2,1)} %param.8) | copy-start | bytes 786436
  74.7 29.5 %copy-start.6 = (bf16[1,32,4096]{2,1,0:T(8,128)(2,1)S(1)}, bf16[1,32,4096]{2,1,0:T(8,128)(2,1)}, u32[]{:S(2)}) copy-start(bf16[1,32,4096]{2,1,0:T(8,128)(2,1)} %param.9) | copy-start | bytes 786436
  74.7 29.5 %copy-start.8 = (f32[1,4096]{1,0:T(1,128)S(1)}, f32[1,4096]{1,0:T(1,128)}, u32[]{:S(2)}) copy-start(f32[1,4096]{1,0:T(1,128)} %refs_4_.1) | copy-start | bytes 49156
  76.3 11.3 %collective-permute-start.17 = (bf16[96,1024]{1,0:T(8,128)(2,1)S(1)}, bf16[96,1024]{1,0:T(8,128)(2,1)S(1)}, u32[]{:S(2)}, u32[]{:S(2)}) collective-permute-start(bf16[96,1024]{1,0:T(8,128)(2,1)S(1)} %get-tuple-element.76), channel_id=1, source_target_pairs={{0,1},{1,0},{2,3},{3,2},{4,5},{5,4},{6,7},{7,6},{8,9},{9,8},{10,11... | collective-permute-start | bytes 589832 | tf_op jit(solution)/shard_map/ppermute | solution.py:292
  80.2 9.5 %collective-permute-start.8 = (bf16[24,1536]{1,0:T(8,128)(2,1)S(1)}, bf16[24,1536]{1,0:T(8,128)(2,1)S(1)}, u32[]{:S(2)}, u32[]{:S(2)}) collective-permute-start(bf16[24,1536]{1,0:T(8,128)(2,1)S(1)} %get-tuple-element.66), channel_id=1, source_target_pairs={{0,2},{1,3},{2,0},{3,1},{4,6},{5,7},{6,4},{7,5},{8,10},{9,11},{10,... | collective-permute-start | bytes 221192 | tf_op jit(solution)/shard_map/ppermute | solution.py:287
  80.9 10.2 %collective-permute-start.9 = (bf16[24,1536]{1,0:T(8,128)(2,1)S(1)}, bf16[24,1536]{1,0:T(8,128)(2,1)S(1)}, u32[]{:S(2)}, u32[]{:S(2)}) collective-permute-start(bf16[24,1536]{1,0:T(8,128)(2,1)S(1)} %get-tuple-element.67), channel_id=1, source_target_pairs={{0,4},{1,5},{2,6},{3,7},{4,0},{5,1},{6,2},{7,3},{8,12},{9,13},{10,... | collective-permute-start | bytes 221192 | tf_op jit(solution)/shard_map/ppermute | solution.py:287
  84.4 7.4 %collective-permute-start.10 = (bf16[24,1536]{1,0:T(8,128)(2,1)S(1)}, bf16[24,1536]{1,0:T(8,128)(2,1)S(1)}, u32[]{:S(2)}, u32[]{:S(2)}) collective-permute-start(bf16[24,1536]{1,0:T(8,128)(2,1)S(1)} %get-tuple-element.68), channel_id=1, source_target_pairs={{0,6},{1,7},{2,4},{3,5},{4,2},{5,3},{6,0},{7,1},{8,14},{9,15},{10,... | collective-permute-start | bytes 221192 | tf_op jit(solution)/shard_map/ppermute | solution.py:287
  85.6 8.6 %collective-permute-start.13 = (bf16[24,1536]{1,0:T(8,128)(2,1)S(1)}, bf16[24,1536]{1,0:T(8,128)(2,1)S(1)}, u32[]{:S(2)}, u32[]{:S(2)}) collective-permute-start(bf16[24,1536]{1,0:T(8,128)(2,1)S(1)} %get-tuple-element.72), channel_id=1, source_target_pairs={{0,2},{1,3},{2,0},{3,1},{4,6},{5,7},{6,4},{7,5},{8,10},{9,11},{10,... | collective-permute-start | bytes 221192 | tf_op jit(solution)/shard_map/ppermute | solution.py:287
  87.6 8.7 %collective-permute-start.14 = (bf16[24,1536]{1,0:T(8,128)(2,1)S(1)}, bf16[24,1536]{1,0:T(8,128)(2,1)S(1)}, u32[]{:S(2)}, u32[]{:S(2)}) collective-permute-start(bf16[24,1536]{1,0:T(8,128)(2,1)S(1)} %get-tuple-element.73), channel_id=1, source_target_pairs={{0,4},{1,5},{2,6},{3,7},{4,0},{5,1},{6,2},{7,3},{8,12},{9,13},{10,... | collective-permute-start | bytes 221192 | tf_op jit(solution)/shard_map/ppermute | solution.py:287
  89.7 6.8 %collective-permute-start.15 = (bf16[24,1536]{1,0:T(8,128)(2,1)S(1)}, bf16[24,1536]{1,0:T(8,128)(2,1)S(1)}, u32[]{:S(2)}, u32[]{:S(2)}) collective-permute-start(bf16[24,1536]{1,0:T(8,128)(2,1)S(1)} %get-tuple-element.74), channel_id=1, source_target_pairs={{0,6},{1,7},{2,4},{3,5},{4,2},{5,3},{6,0},{7,1},{8,14},{9,15},{10,... | collective-permute-start | bytes 221192 | tf_op jit(solution)/shard_map/ppermute | solution.py:287
  91.2 7.1 %collective-permute-start.18 = (bf16[24,1024]{1,0:T(8,128)(2,1)S(1)}, bf16[24,1024]{1,0:T(8,128)(2,1)S(1)}, u32[]{:S(2)}, u32[]{:S(2)}) collective-permute-start(bf16[24,1024]{1,0:T(8,128)(2,1)S(1)} %get-tuple-element.78), channel_id=1, source_target_pairs={{0,2},{1,3},{2,0},{3,1},{4,6},{5,7},{6,4},{7,5},{8,10},{9,11},{10,... | collective-permute-start | bytes 147464 | tf_op jit(solution)/shard_map/ppermute | solution.py:287
  91.8 6.8 %collective-permute-start.19 = (bf16[24,1024]{1,0:T(8,128)(2,1)S(1)}, bf16[24,1024]{1,0:T(8,128)(2,1)S(1)}, u32[]{:S(2)}, u32[]{:S(2)}) collective-permute-start(bf16[24,1024]{1,0:T(8,128)(2,1)S(1)} %get-tuple-element.79), channel_id=1, source_target_pairs={{0,4},{1,5},{2,6},{3,7},{4,0},{5,1},{6,2},{7,3},{8,12},{9,13},{10,... | collective-permute-start | bytes 147464 | tf_op jit(solution)/shard_map/ppermute | solution.py:287
  94.2 5.9 %collective-permute-start.20 = (bf16[24,1024]{1,0:T(8,128)(2,1)S(1)}, bf16[24,1024]{1,0:T(8,128)(2,1)S(1)}, u32[]{:S(2)}, u32[]{:S(2)}) collective-permute-start(bf16[24,1024]{1,0:T(8,128)(2,1)S(1)} %get-tuple-element.80), channel_id=1, source_target_pairs={{0,6},{1,7},{2,4},{3,5},{4,2},{5,3},{6,0},{7,1},{8,14},{9,15},{10,... | collective-permute-start | bytes 147464 | tf_op jit(solution)/shard_map/ppermute | solution.py:287
  96.2 56.1 %slice-start.3 = ((s8[11010048]{0:T(1024)(128)(4,1)}), s8[2621440]{0:T(1024)(128)(4,1)S(1)}, s32[]{:S(2)}) async-start(s8[11010048]{0:T(1024)(128)(4,1)} %bitcast.19), calls=%async_computation.3 | async-start | bytes 5242880
  96.4 7.8 %collective-permute-start.11 = (bf16[32,1536]{1,0:T(8,128)(2,1)S(1)}, bf16[32,1536]{1,0:T(8,128)(2,1)S(1)}, u32[]{:S(2)}, u32[]{:S(2)}) collective-permute-start(bf16[32,1536]{1,0:T(8,128)(2,1)S(1)} %combine.6), channel_id=1, source_target_pairs={{0,8},{8,16},{16,24},{24,0},{1,9},{9,17},{17,25},{25,1},{2,10},{10... | collective-permute-start | bytes 294920 | tf_op jit(solution)/shard_map/ppermute | solution.py:297
  96.6 7.5 %collective-permute-start.16 = (bf16[32,1536]{1,0:T(8,128)(2,1)S(1)}, bf16[32,1536]{1,0:T(8,128)(2,1)S(1)}, u32[]{:S(2)}, u32[]{:S(2)}) collective-permute-start(bf16[32,1536]{1,0:T(8,128)(2,1)S(1)} %combine.7), channel_id=1, source_target_pairs={{0,8},{8,16},{16,24},{24,0},{1,9},{9,17},{17,25},{25,1},{2,10},{10... | collective-permute-start | bytes 294920 | tf_op jit(solution)/shard_map/ppermute | solution.py:297
  100.2 3.9 %collective-permute-start.21 = (bf16[32,1024]{1,0:T(8,128)(2,1)S(1)}, bf16[32,1024]{1,0:T(8,128)(2,1)S(1)}, u32[]{:S(2)}, u32[]{:S(2)}) collective-permute-start(bf16[32,1024]{1,0:T(8,128)(2,1)S(1)} %combine.8), channel_id=1, source_target_pairs={{0,8},{8,16},{16,24},{24,0},{1,9},{9,17},{17,25},{25,1},{2,10},{10... | collective-permute-start | bytes 196616 | tf_op jit(solution)/shard_map/ppermute | solution.py:297
  104.9 9.4 %collective-permute-start.22 = (bf16[24,4096]{1,0:T(8,128)(2,1)S(1)}, bf16[24,4096]{1,0:T(8,128)(2,1)S(1)}, u32[]{:S(2)}, u32[]{:S(2)}) collective-permute-start(bf16[24,4096]{1,0:T(8,128)(2,1)S(1)} %get-tuple-element.84), channel_id=1, source_target_pairs={{0,2},{1,3},{2,0},{3,1},{4,6},{5,7},{6,4},{7,5},{8,10},{9,11},{10,... | collective-permute-start | bytes 589832 | tf_op jit(solution)/shard_map/ppermute | solution.py:287
  105.0 17.2 %collective-permute-start.23 = (bf16[24,4096]{1,0:T(8,128)(2,1)S(1)}, bf16[24,4096]{1,0:T(8,128)(2,1)S(1)}, u32[]{:S(2)}, u32[]{:S(2)}) collective-permute-start(bf16[24,4096]{1,0:T(8,128)(2,1)S(1)} %get-tuple-element.85), channel_id=1, source_target_pairs={{0,4},{1,5},{2,6},{3,7},{4,0},{5,1},{6,2},{7,3},{8,12},{9,13},{10,... | collective-permute-start | bytes 589832 | tf_op jit(solution)/shard_map/ppermute | solution.py:287
  107.0 15.6 %collective-permute-start.24 = (bf16[24,4096]{1,0:T(8,128)(2,1)S(1)}, bf16[24,4096]{1,0:T(8,128)(2,1)S(1)}, u32[]{:S(2)}, u32[]{:S(2)}) collective-permute-start(bf16[24,4096]{1,0:T(8,128)(2,1)S(1)} %get-tuple-element.86), channel_id=1, source_target_pairs={{0,6},{1,7},{2,4},{3,5},{4,2},{5,3},{6,0},{7,1},{8,14},{9,15},{10,... | collective-permute-start | bytes 589832 | tf_op jit(solution)/shard_map/ppermute | solution.py:287
  109.3 14.8 %collective-permute-start.25 = (bf16[24,4096]{1,0:T(8,128)(2,1)S(1)}, bf16[24,4096]{1,0:T(8,128)(2,1)S(1)}, u32[]{:S(2)}, u32[]{:S(2)}) collective-permute-start(bf16[24,4096]{1,0:T(8,128)(2,1)S(1)} %get-tuple-element.83.refs_0_), channel_id=1, source_target_pairs={{0,1},{1,0},{2,3},{3,2},{4,5},{5,4},{6,7},{7,6},{8,9},{9,8},{10,11... | collective-permute-start | bytes 589832 | tf_op jit(solution)/shard_map/ppermute | solution.py:292
  114.3 9.9 %collective-permute-start.26 = (bf16[24,4096]{1,0:T(8,128)(2,1)S(1)}, bf16[24,4096]{1,0:T(8,128)(2,1)S(1)}, u32[]{:S(2)}, u32[]{:S(2)}) collective-permute-start(bf16[24,4096]{1,0:T(8,128)(2,1)S(1)} %collective-permute-done.22.refs_1_), channel_id=1, source_target_pairs={{0,1},{1,0},{2,3},{3,2},{4,5},{5,4},{6,7},{7,6},{8,9},{9,8},{10,11... | collective-permute-start | bytes 589832 | tf_op jit(solution)/shard_map/ppermute | solution.py:292
  122.1 5.7 %collective-permute-start.27 = (bf16[24,4096]{1,0:T(8,128)(2,1)S(1)}, bf16[24,4096]{1,0:T(8,128)(2,1)S(1)}, u32[]{:S(2)}, u32[]{:S(2)}) collective-permute-start(bf16[24,4096]{1,0:T(8,128)(2,1)S(1)} %collective-permute-done.23.refs_2_), channel_id=1, source_target_pairs={{0,1},{1,0},{2,3},{3,2},{4,5},{5,4},{6,7},{7,6},{8,9},{9,8},{10,11... | collective-permute-start | bytes 589832 | tf_op jit(solution)/shard_map/ppermute | solution.py:292
  122.7 7.2 %collective-permute-start.28 = (bf16[24,4096]{1,0:T(8,128)(2,1)S(1)}, bf16[24,4096]{1,0:T(8,128)(2,1)S(1)}, u32[]{:S(2)}, u32[]{:S(2)}) collective-permute-start(bf16[24,4096]{1,0:T(8,128)(2,1)S(1)} %collective-permute-done.24.refs_3_), channel_id=1, source_target_pairs={{0,1},{1,0},{2,3},{3,2},{4,5},{5,4},{6,7},{7,6},{8,9},{9,8},{10,11... | collective-permute-start | bytes 589832 | tf_op jit(solution)/shard_map/ppermute | solution.py:292
  129.9 22.4 %slice-start = ((s8[11010048]{0:T(1024)(128)(4,1)}), s8[4194304]{0:T(1024)(128)(4,1)S(1)}, s32[]{:S(2)}) async-start(s8[11010048]{0:T(1024)(128)(4,1)} %bitcast.17), calls=%async_computation | async-start | bytes 8388608
  129.9 22.4 %slice-start.6 = ((s8[7340032]{0:T(1024)(128)(4,1)}), s8[4194304]{0:T(1024)(128)(4,1)S(1)}, s32[]{:S(2)}) async-start(s8[7340032]{0:T(1024)(128)(4,1)} %bitcast.21), calls=%async_computation.6 | async-start | bytes 8388608
  130.0 22.3 %slice-start.1 = ((s8[11010048]{0:T(1024)(128)(4,1)}), s8[4194304]{0:T(1024)(128)(4,1)S(1)}, s32[]{:S(2)}) async-start(s8[11010048]{0:T(1024)(128)(4,1)} %bitcast.17), calls=%async_computation.1 | async-start | bytes 8388608
  130.0 22.3 %slice-start.2 = ((s8[11010048]{0:T(1024)(128)(4,1)}), s8[2621440]{0:T(1024)(128)(4,1)S(1)}, s32[]{:S(2)}) async-start(s8[11010048]{0:T(1024)(128)(4,1)} %bitcast.17), calls=%async_computation.2 | async-start | bytes 5242880
  130.0 22.3 %slice-start.4 = ((s8[11010048]{0:T(1024)(128)(4,1)}), s8[4194304]{0:T(1024)(128)(4,1)S(1)}, s32[]{:S(2)}) async-start(s8[11010048]{0:T(1024)(128)(4,1)} %bitcast.19), calls=%async_computation.4 | async-start | bytes 8388608
  130.1 22.3 %slice-start.5 = ((s8[11010048]{0:T(1024)(128)(4,1)}), s8[4194304]{0:T(1024)(128)(4,1)S(1)}, s32[]{:S(2)}) async-start(s8[11010048]{0:T(1024)(128)(4,1)} %bitcast.19), calls=%async_computation.5 | async-start | bytes 8388608
  130.1 22.3 %slice-start.7 = ((s8[7340032]{0:T(1024)(128)(4,1)}), s8[3145728]{0:T(1024)(128)(4,1)S(1)}, s32[]{:S(2)}) async-start(s8[7340032]{0:T(1024)(128)(4,1)} %bitcast.21), calls=%async_computation.7 | async-start | bytes 6291456
  154.7 8.4 %collective-permute-start.29 = (bf16[96,1536]{1,0:T(8,128)(2,1)S(1)}, bf16[96,1536]{1,0:T(8,128)(2,1)S(1)}, u32[]{:S(2)}, u32[]{:S(2)}) collective-permute-start(bf16[96,1536]{1,0:T(8,128)(2,1)S(1)} %get-tuple-element.90), channel_id=1, source_target_pairs={{0,1},{1,0},{2,3},{3,2},{4,5},{5,4},{6,7},{7,6},{8,9},{9,8},{10,11... | collective-permute-start | bytes 884744 | tf_op jit(solution)/shard_map/ppermute | solution.py:292
  157.6 19.4 %collective-permute-start.34 = (bf16[96,1536]{1,0:T(8,128)(2,1)S(1)}, bf16[96,1536]{1,0:T(8,128)(2,1)S(1)}, u32[]{:S(2)}, u32[]{:S(2)}) collective-permute-start(bf16[96,1536]{1,0:T(8,128)(2,1)S(1)} %get-tuple-element.96), channel_id=1, source_target_pairs={{0,1},{1,0},{2,3},{3,2},{4,5},{5,4},{6,7},{7,6},{8,9},{9,8},{10,11... | collective-permute-start | bytes 884744 | tf_op jit(solution)/shard_map/ppermute | solution.py:292
  160.8 7.6 %collective-permute-start.39 = (bf16[96,1024]{1,0:T(8,128)(2,1)S(1)}, bf16[96,1024]{1,0:T(8,128)(2,1)S(1)}, u32[]{:S(2)}, u32[]{:S(2)}) collective-permute-start(bf16[96,1024]{1,0:T(8,128)(2,1)S(1)} %get-tuple-element.102), channel_id=1, source_target_pairs={{0,1},{1,0},{2,3},{3,2},{4,5},{5,4},{6,7},{7,6},{8,9},{9,8},{10,11... | collective-permute-start | bytes 589832 | tf_op jit(solution)/shard_map/ppermute | solution.py:292
  163.1 23.4 %collective-permute-start.30 = (bf16[24,1536]{1,0:T(8,128)(2,1)S(1)}, bf16[24,1536]{1,0:T(8,128)(2,1)S(1)}, u32[]{:S(2)}, u32[]{:S(2)}) collective-permute-start(bf16[24,1536]{1,0:T(8,128)(2,1)S(1)} %get-tuple-element.92), channel_id=1, source_target_pairs={{0,2},{1,3},{2,0},{3,1},{4,6},{5,7},{6,4},{7,5},{8,10},{9,11},{10,... | collective-permute-start | bytes 221192 | tf_op jit(solution)/shard_map/ppermute | solution.py:287
  168.4 9.2 %collective-permute-start.40 = (bf16[24,1024]{1,0:T(8,128)(2,1)S(1)}, bf16[24,1024]{1,0:T(8,128)(2,1)S(1)}, u32[]{:S(2)}, u32[]{:S(2)}) collective-permute-start(bf16[24,1024]{1,0:T(8,128)(2,1)S(1)} %get-tuple-element.104), channel_id=1, source_target_pairs={{0,2},{1,3},{2,0},{3,1},{4,6},{5,7},{6,4},{7,5},{8,10},{9,11},{10,... | collective-permute-start | bytes 147464 | tf_op jit(solution)/shard_map/ppermute | solution.py:287
  174.6 10.3 %collective-permute-start.41 = (bf16[24,1024]{1,0:T(8,128)(2,1)S(1)}, bf16[24,1024]{1,0:T(8,128)(2,1)S(1)}, u32[]{:S(2)}, u32[]{:S(2)}) collective-permute-start(bf16[24,1024]{1,0:T(8,128)(2,1)S(1)} %get-tuple-element.105), channel_id=1, source_target_pairs={{0,4},{1,5},{2,6},{3,7},{4,0},{5,1},{6,2},{7,3},{8,12},{9,13},{10,... | collective-permute-start | bytes 147464 | tf_op jit(solution)/shard_map/ppermute | solution.py:287
  174.6 10.3 %collective-permute-start.42 = (bf16[24,1024]{1,0:T(8,128)(2,1)S(1)}, bf16[24,1024]{1,0:T(8,128)(2,1)S(1)}, u32[]{:S(2)}, u32[]{:S(2)}) collective-permute-start(bf16[24,1024]{1,0:T(8,128)(2,1)S(1)} %get-tuple-element.106), channel_id=1, source_target_pairs={{0,6},{1,7},{2,4},{3,5},{4,2},{5,3},{6,0},{7,1},{8,14},{9,15},{10,... | collective-permute-start | bytes 147464 | tf_op jit(solution)/shard_map/ppermute | solution.py:287
  177.0 13.0 %collective-permute-start.31 = (bf16[24,1536]{1,0:T(8,128)(2,1)S(1)}, bf16[24,1536]{1,0:T(8,128)(2,1)S(1)}, u32[]{:S(2)}, u32[]{:S(2)}) collective-permute-start(bf16[24,1536]{1,0:T(8,128)(2,1)S(1)} %get-tuple-element.93), channel_id=1, source_target_pairs={{0,4},{1,5},{2,6},{3,7},{4,0},{5,1},{6,2},{7,3},{8,12},{9,13},{10,... | collective-permute-start | bytes 221192 | tf_op jit(solution)/shard_map/ppermute | solution.py:287
  177.6 12.5 %collective-permute-start.32 = (bf16[24,1536]{1,0:T(8,128)(2,1)S(1)}, bf16[24,1536]{1,0:T(8,128)(2,1)S(1)}, u32[]{:S(2)}, u32[]{:S(2)}) collective-permute-start(bf16[24,1536]{1,0:T(8,128)(2,1)S(1)} %get-tuple-element.94), channel_id=1, source_target_pairs={{0,6},{1,7},{2,4},{3,5},{4,2},{5,3},{6,0},{7,1},{8,14},{9,15},{10,... | collective-permute-start | bytes 221192 | tf_op jit(solution)/shard_map/ppermute | solution.py:287
  184.9 6.0 %collective-permute-start.35 = (bf16[24,1536]{1,0:T(8,128)(2,1)S(1)}, bf16[24,1536]{1,0:T(8,128)(2,1)S(1)}, u32[]{:S(2)}, u32[]{:S(2)}) collective-permute-start(bf16[24,1536]{1,0:T(8,128)(2,1)S(1)} %get-tuple-element.98), channel_id=1, source_target_pairs={{0,2},{1,3},{2,0},{3,1},{4,6},{5,7},{6,4},{7,5},{8,10},{9,11},{10,... | collective-permute-start | bytes 221192 | tf_op jit(solution)/shard_map/ppermute | solution.py:287
  184.9 6.0 %collective-permute-start.36 = (bf16[24,1536]{1,0:T(8,128)(2,1)S(1)}, bf16[24,1536]{1,0:T(8,128)(2,1)S(1)}, u32[]{:S(2)}, u32[]{:S(2)}) collective-permute-start(bf16[24,1536]{1,0:T(8,128)(2,1)S(1)} %get-tuple-element.99), channel_id=1, source_target_pairs={{0,4},{1,5},{2,6},{3,7},{4,0},{5,1},{6,2},{7,3},{8,12},{9,13},{10,... | collective-permute-start | bytes 221192 | tf_op jit(solution)/shard_map/ppermute | solution.py:287
  186.5 6.2 %collective-permute-start.37 = (bf16[24,1536]{1,0:T(8,128)(2,1)S(1)}, bf16[24,1536]{1,0:T(8,128)(2,1)S(1)}, u32[]{:S(2)}, u32[]{:S(2)}) collective-permute-start(bf16[24,1536]{1,0:T(8,128)(2,1)S(1)} %get-tuple-element.100), channel_id=1, source_target_pairs={{0,6},{1,7},{2,4},{3,5},{4,2},{5,3},{6,0},{7,1},{8,14},{9,15},{10,... | collective-permute-start | bytes 221192 | tf_op jit(solution)/shard_map/ppermute | solution.py:287
  190.0 3.7 %collective-permute-start.43 = (bf16[32,1024]{1,0:T(8,128)(2,1)S(1)}, bf16[32,1024]{1,0:T(8,128)(2,1)S(1)}, u32[]{:S(2)}, u32[]{:S(2)}) collective-permute-start(bf16[32,1024]{1,0:T(8,128)(2,1)S(1)} %combine.11), channel_id=1, source_target_pairs={{0,8},{8,16},{16,24},{24,0},{1,9},{9,17},{17,25},{25,1},{2,10},{10... | collective-permute-start | bytes 196616 | tf_op jit(solution)/shard_map/ppermute | solution.py:297
  190.3 4.5 %collective-permute-start.33 = (bf16[32,1536]{1,0:T(8,128)(2,1)S(1)}, bf16[32,1536]{1,0:T(8,128)(2,1)S(1)}, u32[]{:S(2)}, u32[]{:S(2)}) collective-permute-start(bf16[32,1536]{1,0:T(8,128)(2,1)S(1)} %combine.9), channel_id=1, source_target_pairs={{0,8},{8,16},{16,24},{24,0},{1,9},{9,17},{17,25},{25,1},{2,10},{10... | collective-permute-start | bytes 294920 | tf_op jit(solution)/shard_map/ppermute | solution.py:297
  192.9 4.1 %collective-permute-start.38 = (bf16[32,1536]{1,0:T(8,128)(2,1)S(1)}, bf16[32,1536]{1,0:T(8,128)(2,1)S(1)}, u32[]{:S(2)}, u32[]{:S(2)}) collective-permute-start(bf16[32,1536]{1,0:T(8,128)(2,1)S(1)} %combine.10), channel_id=1, source_target_pairs={{0,8},{8,16},{16,24},{24,0},{1,9},{9,17},{17,25},{25,1},{2,10},{10... | collective-permute-start | bytes 294920 | tf_op jit(solution)/shard_map/ppermute | solution.py:297

commit v2 on v1

--- a/solution.py
+++ b/solution.py
@@ -11,6 +11,8 @@
 CAP = 24
 SPAN = EXPERTS * CAP
 EIGHTHS = (3, 3, 2)
+TURNS = (1, 3, 2)
+RETURNS = (3, 2, 1)
 MIB = 1 << 20
 epsilon = 1e-05
 
@@ -303,7 +305,7 @@
     normed, *routed = route(t, x_parts, arriving, scale, chosen)
     x = x_parts[0] if arriving is None else routed.pop()
     mine = [None] * EXPERTS
-    for k in (3, 2, 1, 0):
+    for k in (*TURNS, 0):
         mine[k] = over_experts(routed[k], k)
     pieces = list(mine)
     for m in range(1, group):
@@ -327,7 +329,7 @@
         after = [own]
         others = [over_group(other, -m) for m, other in enumerate(others, 1)]
         back = list(merge(own, others))
-        for k in (3, 2, 1):
+        for k in RETURNS:
             back[k] = over_experts(back[k], k)
         out = combine(table, x, back, start)
         outs.append(over_sections(out))

time: 198 us -> 198 us (level)
  no operation moved by 1% of the time
where the time goes in v2:
time: 198 us
  Pallas kernels  78.7 us (40%)
  starting transfers between devices  58.4 us (29%)
  waiting for transfers between devices  48.7 us (25%)
  local copies, waits for them, and re-layouts  10.7 us (5%)
    pallas_call x30, Pallas kernels, call(): pl.pallas_call(body, in_specs=list(specs) + [WHOLE] * len(keep) + [HBM] *...  78.7 us
    ppermute x24, starting transfers between devices, over_experts(): lax.ppermute(v, 'expert', [(e * group + j, (e ^ k) * group + j) for e in...  43 us
    ppermute x14, waiting for transfers between devices, over_group(): lax.ppermute(v, 'expert', [(e * group + j, e * group + (j + m) % group) f...  21.4 us
    ppermute x24, waiting for transfers between devices, over_experts(): lax.ppermute(v, 'expert', [(e * group + j, (e ^ k) * group + j) for e in...  19.6 us
    ppermute x14, starting transfers between devices, over_group(): lax.ppermute(v, 'expert', [(e * group + j, e * group + (j + m) % group) f...  12.7 us
    unnamed x36, local copies, waits for them, and re-layouts  9.92 us
    ppermute x6, waiting for transfers between devices, over_sections(): return lax.ppermute(v, 'section', [(i, (i + 1) % n) for i in range(n)])  7.68 us
  transfers between devices with their start and end apart: 44, of which 20 were waited for; matrix products, arithmetic and copies ran while one was open for 0% of the time, Pallas kernels for 17%

profile of v2, /device:TPU:0, one launch (start us, length us, event | category | flops | bytes accessed | tf_op | source)
XLA Modules:
  0.0 197.8 jit_solution(4857357649692443319)
XLA Ops:
  0.0 0.8 copy.9.refs_2_.refs_5_
  0.8 0.9 copy-done.4
  1.7 0.7 copy-done.7
  2.4 0.7 route.2
  3.1 3.1 %collective-permute-start = (bf16[24,4096]{1,0:T(8,128)(2,1)S(1)}, bf16[24,4096]{1,0:T(8,128)(2,1)S(1)}, u32[]{:S(2)}, u32[]{:S(2)}) collective-permute-start(bf16[24,4096]{1,0:T(8,128)(2,1)S(1)} %get-tuple-element.58), channel_id=1, source_target_pairs={{0,2},{1,3},{2,0},{3,1},{4,6},{5,7},{6,4},{7,5},{8,10},{9,11},{10,... | collective-permute-start | bytes 589832 | tf_op jit(solution)/shard_map/ppermute | solution.py:289
  6.3 2.6 %collective-permute-start.1 = (bf16[24,4096]{1,0:T(8,128)(2,1)S(1)}, bf16[24,4096]{1,0:T(8,128)(2,1)S(1)}, u32[]{:S(2)}, u32[]{:S(2)}) collective-permute-start(bf16[24,4096]{1,0:T(8,128)(2,1)S(1)} %get-tuple-element.59), channel_id=1, source_target_pairs={{0,4},{1,5},{2,6},{3,7},{4,0},{5,1},{6,2},{7,3},{8,12},{9,13},{10,... | collective-permute-start | bytes 589832 | tf_op jit(solution)/shard_map/ppermute | solution.py:289
  8.8 1.7 collective-permute-start.3
  10.5 4.1 %fetch.6.refs_3_.refs_1_.refs_4_ = bf16[3584,1536]{1,0:T(8,128)(2,1)S(1)} custom-call(bf16[3584,4096]{1,0:T(8,128)(2,1)} %bitcast.30, bf16[24,4096]{1,0:T(8,128)(2,1)S(1)} %get-tuple-element.57.refs_0_.refs_1_), custom_call_target="tpu_custom_call" | custom-call | flops 1651507200 | bytes 22020096 | tf_op jit(solution)/shard_map/fetch/pallas_call | solution.py:44
  14.7 7.1 %fetch.7.refs_4_.refs_1_ = bf16[3584,1024]{1,0:T(8,128)(2,1)S(1)} custom-call(bf16[3584,4096]{1,0:T(8,128)(2,1)} %bitcast.31, bf16[24,4096]{1,0:T(8,128)(2,1)S(1)} %get-tuple-element.57.refs_0_.refs_1_), custom_call_target="tpu_custom_call" | custom-call | flops 1101004800 | bytes 14680064 | tf_op jit(solution)/shard_map/fetch/pallas_call | solution.py:44
  21.7 6.8 %fetch.5.refs_1_.refs_3_ = bf16[3584,1536]{1,0:T(8,128)(2,1)S(1)} custom-call(bf16[3584,4096]{1,0:T(8,128)(2,1)} %bitcast.32, bf16[24,4096]{1,0:T(8,128)(2,1)S(1)} %get-tuple-element.57.refs_0_.refs_1_), custom_call_target="tpu_custom_call" | custom-call | flops 1651507200 | bytes 22020096 | tf_op jit(solution)/shard_map/fetch/pallas_call | solution.py:44
  28.5 4.1 %copy-done.1 = bf16[3584,1536]{1,0:T(8,128)(2,1)} copy-done((bf16[3584,1536]{1,0:T(8,128)(2,1)}, bf16[3584,1536]{1,0:T(8,128)(2,1)S(1)}, u32[]{:S(2)}) %copy-start.1) | copy-done | bytes 11010072
  32.9 1.7 collective-permute-start.5
  34.9 5.2 %fetch.4.refs_2_ = bf16[2048,3584]{1,0:T(8,128)(2,1)S(1)} custom-call(bf16[4096,3584]{1,0:T(8,128)(2,1)} %bitcast.33, bf16[24,4096]{1,0:T(8,128)(2,1)S(1)} %get-tuple-element.57.refs_0_.refs_1_), custom_call_target="tpu_custom_call" | custom-call | flops 2202009600 | bytes 29360128 | tf_op jit(solution)/shard_map/fetch/pallas_call | solution.py:44
  40.4 4.1 %collective-permute-done.5.refs_6_ = bf16[24,4096]{1,0:T(8,128)(2,1)S(1)} collective-permute-done((bf16[24,4096]{1,0:T(8,128)(2,1)S(1)}, bf16[24,4096]{1,0:T(8,128)(2,1)S(1)}, u32[]{:S(2)}, u32[]{:S(2)}) %collective-permute-start.5) | collective-permute-done | bytes 196640 | tf_op jit(solution)/shard_map/ppermute | solution.py:294
  44.5 2.1 %collective-permute-done.6.refs_7_ = bf16[24,4096]{1,0:T(8,128)(2,1)S(1)} collective-permute-done((bf16[24,4096]{1,0:T(8,128)(2,1)S(1)}, bf16[24,4096]{1,0:T(8,128)(2,1)S(1)}, u32[]{:S(2)}, u32[]{:S(2)}) %collective-permute-start.6) | collective-permute-done | bytes 196640 | tf_op jit(solution)/shard_map/ppermute | solution.py:294
  46.7 17.1 %expand.2.refs_0_ = bf16[192,3584]{1,0:T(8,128)(2,1)S(1)} custom-call(bf16[192,2048]{1,0:T(8,128)(2,1)S(1)} %get-tuple-element.61.refs_0_, bf16[192,2048]{1,0:T(8,128)(2,1)S(1)} %get-tuple-element.62.refs_1_, bf16[2048,3584]{1,0:T(8,128)(2,1)S(1)} %fetch.4.refs_2_, bf16[4096,3584]{1,0:T(8,128)(2,1)} %bitcast.34, bf16[4096,3584]{1,0:T(8,128)(2,1)} %bitcast.36), custom_call_target="tpu_custom_call" | custom-call | flops 11274289152 | bytes 29360128 | tf_op jit(solution)/shard_map/expand/pallas_call | solution.py:44
  63.8 4.1 %copy-done.2 = bf16[3584,1536]{1,0:T(8,128)(2,1)S(1)} copy-done((bf16[3584,1536]{1,0:T(8,128)(2,1)S(1)}, bf16[3584,1536]{1,0:T(8,128)(2,1)}, u32[]{:S(2)}) %copy-start.2) | copy-done | bytes 11010072
  67.9 2.3 %contract.6 = (f32[96,1536]{1,0:T(8,128)S(1)}, bf16[96,1536]{1,0:T(8,128)(2,1)S(1)}) custom-call(bf16[192,3584]{1,0:T(8,128)(2,1)S(1)} %expand.2.refs_0_, bf16[3584,1536]{1,0:T(8,128)(2,1)S(1)} %copy-done.2, bf16[2048,3584]{1,0:T(8,128)(2,1)S(1)} %fetch.4.refs_2_, bf16[3584,1536]{1,0:T(8,128)(2,1)S(1)} %fetch.6.refs_3_.refs_1_.refs_4_, ...), custom_call_target="tpu_custom_call" | custom-call | flops 2113929216 | bytes 11010048 | tf_op jit(solution)/shard_map/contract/pallas_call | solution.py:44
  70.8 2.3 %contract.7 = (f32[96,1536]{1,0:T(8,128)S(1)}, bf16[96,1536]{1,0:T(8,128)(2,1)S(1)}) custom-call(bf16[192,3584]{1,0:T(8,128)(2,1)S(1)} %expand.2.refs_0_, bf16[3584,1536]{1,0:T(8,128)(2,1)S(1)} %fetch.6.refs_3_.refs_1_.refs_4_, bf16[2048,3584]{1,0:T(8,128)(2,1)S(1)} %fetch.4.refs_2_, bf16[3584,1536]{1,0:T(8,128)(2,1)S(1)} %copy-done.2, ...), custom_call_target="tpu_custom_call" | custom-call | flops 2113929216 | bytes 11010048 | tf_op jit(solution)/shard_map/contract/pallas_call | solution.py:44
  73.1 1.6 collective-permute-start.12
  74.7 1.6 contract.8
  76.9 3.2 %collective-permute-done.7.refs_1_ = bf16[96,1536]{1,0:T(8,128)(2,1)S(1)} collective-permute-done((bf16[96,1536]{1,0:T(8,128)(2,1)S(1)}, bf16[96,1536]{1,0:T(8,128)(2,1)S(1)}, u32[]{:S(2)}, u32[]{:S(2)}) %collective-permute-start.7) | collective-permute-done | bytes 294944 | tf_op jit(solution)/shard_map/ppermute | solution.py:294
  80.2 0.7 collective-permute-start.8
  80.9 3.5 %collective-permute-start.9 = (bf16[24,1536]{1,0:T(8,128)(2,1)S(1)}, bf16[24,1536]{1,0:T(8,128)(2,1)S(1)}, u32[]{:S(2)}, u32[]{:S(2)}) collective-permute-start(bf16[24,1536]{1,0:T(8,128)(2,1)S(1)} %get-tuple-element.67), channel_id=1, source_target_pairs={{0,4},{1,5},{2,6},{3,7},{4,0},{5,1},{6,2},{7,3},{8,12},{9,13},{10,... | collective-permute-start | bytes 221192 | tf_op jit(solution)/shard_map/ppermute | solution.py:289
  84.7 0.9 collective-permute-done.12.refs_1_
  85.6 0.6 collective-permute-start.13
  86.2 1.4 collective-permute-done.17.refs_1_
  87.6 2.0 %collective-permute-start.14 = (bf16[24,1536]{1,0:T(8,128)(2,1)S(1)}, bf16[24,1536]{1,0:T(8,128)(2,1)S(1)}, u32[]{:S(2)}, u32[]{:S(2)}) collective-permute-start(bf16[24,1536]{1,0:T(8,128)(2,1)S(1)} %get-tuple-element.73), channel_id=1, source_target_pairs={{0,4},{1,5},{2,6},{3,7},{4,0},{5,1},{6,2},{7,3},{8,12},{9,13},{10,... | collective-permute-start | bytes 221192 | tf_op jit(solution)/shard_map/ppermute | solution.py:289
  89.7 1.4 collective-permute-start.15
  91.2 0.6 collective-permute-start.18
  91.8 2.4 %collective-permute-start.19 = (bf16[24,1024]{1,0:T(8,128)(2,1)S(1)}, bf16[24,1024]{1,0:T(8,128)(2,1)S(1)}, u32[]{:S(2)}, u32[]{:S(2)}) collective-permute-start(bf16[24,1024]{1,0:T(8,128)(2,1)S(1)} %get-tuple-element.79), channel_id=1, source_target_pairs={{0,4},{1,5},{2,6},{3,7},{4,0},{5,1},{6,2},{7,3},{8,12},{9,13},{10,... | collective-permute-start | bytes 147464 | tf_op jit(solution)/shard_map/ppermute | solution.py:289
  94.2 1.4 collective-permute-start.20
  96.6 1.7 collective-permute-start.16
  98.6 1.5 collective-permute-done.20.refs_5_
  100.5 3.7 %collective-permute-done.21.refs_2_ = bf16[32,1024]{1,0:T(8,128)(2,1)S(1)} collective-permute-done((bf16[32,1024]{1,0:T(8,128)(2,1)S(1)}, bf16[32,1024]{1,0:T(8,128)(2,1)S(1)}, u32[]{:S(2)}, u32[]{:S(2)}) %collective-permute-start.21) | collective-permute-done | bytes 65568 | tf_op jit(solution)/shard_map/ppermute | solution.py:299
  104.2 0.7 route.3
  105.0 2.1 %collective-permute-start.23 = (bf16[24,4096]{1,0:T(8,128)(2,1)S(1)}, bf16[24,4096]{1,0:T(8,128)(2,1)S(1)}, u32[]{:S(2)}, u32[]{:S(2)}) collective-permute-start(bf16[24,4096]{1,0:T(8,128)(2,1)S(1)} %get-tuple-element.85), channel_id=1, source_target_pairs={{0,4},{1,5},{2,6},{3,7},{4,0},{5,1},{6,2},{7,3},{8,12},{9,13},{10,... | collective-permute-start | bytes 589832 | tf_op jit(solution)/shard_map/ppermute | solution.py:289
  107.0 2.3 %collective-permute-start.24 = (bf16[24,4096]{1,0:T(8,128)(2,1)S(1)}, bf16[24,4096]{1,0:T(8,128)(2,1)S(1)}, u32[]{:S(2)}, u32[]{:S(2)}) collective-permute-start(bf16[24,4096]{1,0:T(8,128)(2,1)S(1)} %get-tuple-element.86), channel_id=1, source_target_pairs={{0,6},{1,7},{2,4},{3,5},{4,2},{5,3},{6,0},{7,1},{8,14},{9,15},{10,... | collective-permute-start | bytes 589832 | tf_op jit(solution)/shard_map/ppermute | solution.py:289
  109.9 4.4 %collective-permute-done.22.refs_1_ = bf16[24,4096]{1,0:T(8,128)(2,1)S(1)} collective-permute-done((bf16[24,4096]{1,0:T(8,128)(2,1)S(1)}, bf16[24,4096]{1,0:T(8,128)(2,1)S(1)}, u32[]{:S(2)}, u32[]{:S(2)}) %collective-permute-start.22) | collective-permute-done | bytes 196640 | tf_op jit(solution)/shard_map/ppermute | solution.py:289
  114.8 7.3 %collective-permute-done.23.refs_2_ = bf16[24,4096]{1,0:T(8,128)(2,1)S(1)} collective-permute-done((bf16[24,4096]{1,0:T(8,128)(2,1)S(1)}, bf16[24,4096]{1,0:T(8,128)(2,1)S(1)}, u32[]{:S(2)}, u32[]{:S(2)}) %collective-permute-start.23) | collective-permute-done | bytes 196640 | tf_op jit(solution)/shard_map/ppermute | solution.py:289
  122.7 1.5 collective-permute-start.28
  124.2 3.6 %collective-permute-done.27.refs_6_ = bf16[24,4096]{1,0:T(8,128)(2,1)S(1)} collective-permute-done((bf16[24,4096]{1,0:T(8,128)(2,1)S(1)}, bf16[24,4096]{1,0:T(8,128)(2,1)S(1)}, u32[]{:S(2)}, u32[]{:S(2)}) %collective-permute-start.27) | collective-permute-done | bytes 196640 | tf_op jit(solution)/shard_map/ppermute | solution.py:294
  127.8 2.1 %collective-permute-done.28.refs_7_ = bf16[24,4096]{1,0:T(8,128)(2,1)S(1)} collective-permute-done((bf16[24,4096]{1,0:T(8,128)(2,1)S(1)}, bf16[24,4096]{1,0:T(8,128)(2,1)S(1)}, u32[]{:S(2)}, u32[]{:S(2)}) %collective-permute-start.28) | collective-permute-done | bytes 196640 | tf_op jit(solution)/shard_map/ppermute | solution.py:294
  130.1 22.2 %expand.3.refs_0_ = bf16[192,3584]{1,0:T(8,128)(2,1)S(1)} custom-call(bf16[192,2048]{1,0:T(8,128)(2,1)S(1)} %get-tuple-element.87.refs_0_, bf16[192,2048]{1,0:T(8,128)(2,1)S(1)} %get-tuple-element.88.refs_1_, bf16[2048,3584]{1,0:T(8,128)(2,1)S(1)} %fetch.4.refs_2_, bf16[4096,3584]{1,0:T(8,128)(2,1)} %bitcast.35, bf16[4096,3584]{1,0:T(8,128)(2,1)} %bitcast.37), custom_call_target="tpu_custom_call" | custom-call | flops 11274289152 | bytes 29360128 | tf_op jit(solution)/shard_map/expand/pallas_call | solution.py:44
  152.4 2.3 %contract.9 = (f32[96,1536]{1,0:T(8,128)S(1)}, bf16[96,1536]{1,0:T(8,128)(2,1)S(1)}) custom-call(bf16[192,3584]{1,0:T(8,128)(2,1)S(1)} %expand.3.refs_0_, bf16[3584,1536]{1,0:T(8,128)(2,1)S(1)} %bitcast.20, bf16[2048,3584]{1,0:T(8,128)(2,1)S(1)} %fetch.4.refs_2_, bf16[3584,1536]{1,0:T(8,128)(2,1)S(1)} %bitcast.18, bf16[3584,1024]{1,0:T(8,128)(2,1)S(1)} %bitcast.22), custom_call_target="tpu_custom_call" | custom-call | flops 2113929216 | bytes 11010048 | tf_op jit(solution)/shard_map/contract/pallas_call | solution.py:44
  155.3 2.3 %contract.10 = (f32[96,1536]{1,0:T(8,128)S(1)}, bf16[96,1536]{1,0:T(8,128)(2,1)S(1)}) custom-call(bf16[192,3584]{1,0:T(8,128)(2,1)S(1)} %expand.3.refs_0_, bf16[3584,1536]{1,0:T(8,128)(2,1)S(1)} %bitcast.18, bf16[2048,3584]{1,0:T(8,128)(2,1)S(1)} %fetch.4.refs_2_, bf16[3584,1536]{1,0:T(8,128)(2,1)S(1)} %bitcast.20, bf16[3584,1024]{1,0:T(8,128)(2,1)S(1)} %bitcast.22, ...), custom_call_target="tpu_custom_call" | custom-call | flops 2113929216 | bytes 11010048 | tf_op jit(solution)/shard_map/contract/pallas_call | solution.py:44
  157.6 1.6 collective-permute-start.34
  159.2 1.6 contract.11
  160.8 0.6 collective-permute-start.39
  161.4 1.7 collective-permute-done.29.refs_1_
  163.1 3.3 %collective-permute-start.30 = (bf16[24,1536]{1,0:T(8,128)(2,1)S(1)}, bf16[24,1536]{1,0:T(8,128)(2,1)S(1)}, u32[]{:S(2)}, u32[]{:S(2)}) collective-permute-start(bf16[24,1536]{1,0:T(8,128)(2,1)S(1)} %get-tuple-element.92), channel_id=1, source_target_pairs={{0,2},{1,3},{2,0},{3,1},{4,6},{5,7},{6,4},{7,5},{8,10},{9,11},{10,... | collective-permute-start | bytes 221192 | tf_op jit(solution)/shard_map/ppermute | solution.py:289
  166.4 1.9 collective-permute-done.39.refs_1_
  168.4 6.2 %collective-permute-start.40 = (bf16[24,1024]{1,0:T(8,128)(2,1)S(1)}, bf16[24,1024]{1,0:T(8,128)(2,1)S(1)}, u32[]{:S(2)}, u32[]{:S(2)}) collective-permute-start(bf16[24,1024]{1,0:T(8,128)(2,1)S(1)} %get-tuple-element.104), channel_id=1, source_target_pairs={{0,2},{1,3},{2,0},{3,1},{4,6},{5,7},{6,4},{7,5},{8,10},{9,11},{10,... | collective-permute-start | bytes 147464 | tf_op jit(solution)/shard_map/ppermute | solution.py:289
  174.6 2.4 %collective-permute-start.42 = (bf16[24,1024]{1,0:T(8,128)(2,1)S(1)}, bf16[24,1024]{1,0:T(8,128)(2,1)S(1)}, u32[]{:S(2)}, u32[]{:S(2)}) collective-permute-start(bf16[24,1024]{1,0:T(8,128)(2,1)S(1)} %get-tuple-element.106), channel_id=1, source_target_pairs={{0,6},{1,7},{2,4},{3,5},{4,2},{5,3},{6,0},{7,1},{8,14},{9,15},{10,... | collective-permute-start | bytes 147464 | tf_op jit(solution)/shard_map/ppermute | solution.py:289
  177.6 3.0 %collective-permute-start.32 = (bf16[24,1536]{1,0:T(8,128)(2,1)S(1)}, bf16[24,1536]{1,0:T(8,128)(2,1)S(1)}, u32[]{:S(2)}, u32[]{:S(2)}) collective-permute-start(bf16[24,1536]{1,0:T(8,128)(2,1)S(1)} %get-tuple-element.94), channel_id=1, source_target_pairs={{0,6},{1,7},{2,4},{3,5},{4,2},{5,3},{6,0},{7,1},{8,14},{9,15},{10,... | collective-permute-start | bytes 221192 | tf_op jit(solution)/shard_map/ppermute | solution.py:289
  180.6 4.4 %collective-permute-done.41.refs_4_ = bf16[24,1024]{1,0:T(8,128)(2,1)S(1)} collective-permute-done((bf16[24,1024]{1,0:T(8,128)(2,1)S(1)}, bf16[24,1024]{1,0:T(8,128)(2,1)S(1)}, u32[]{:S(2)}, u32[]{:S(2)}) %collective-permute-start.41) | collective-permute-done | bytes 49184 | tf_op jit(solution)/shard_map/ppermute | solution.py:289
  184.9 1.6 collective-permute-start.36
  186.5 2.8 %collective-permute-start.37 = (bf16[24,1536]{1,0:T(8,128)(2,1)S(1)}, bf16[24,1536]{1,0:T(8,128)(2,1)S(1)}, u32[]{:S(2)}, u32[]{:S(2)}) collective-permute-start(bf16[24,1536]{1,0:T(8,128)(2,1)S(1)} %get-tuple-element.100), channel_id=1, source_target_pairs={{0,6},{1,7},{2,4},{3,5},{4,2},{5,3},{6,0},{7,1},{8,14},{9,15},{10,... | collective-permute-start | bytes 221192 | tf_op jit(solution)/shard_map/ppermute | solution.py:289
  190.3 0.6 collective-permute-start.33
  190.9 1.7 collective-permute-done.37.refs_5_
  192.9 0.8 collective-permute-done.43
  193.8 1.1 collective-permute-done.33
  194.8 2.1 %collective-permute-done.38 = bf16[32,1536]{1,0:T(8,128)(2,1)S(1)} collective-permute-done((bf16[32,1536]{1,0:T(8,128)(2,1)S(1)}, bf16[32,1536]{1,0:T(8,128)(2,1)S(1)}, u32[]{:S(2)}, u32[]{:S(2)}) %collective-permute-start.38) | collective-permute-done | bytes 98336 | tf_op jit(solution)/shard_map/ppermute | solution.py:299
  197.0 0.8 maximum_bitcast_fusion
  (97 shorter events, 8.6 us)
Async XLA Ops:
  0.8 1.0 copy-start.4
  1.7 0.7 copy-start.7
  3.1 29.5 %collective-permute-start = (bf16[24,4096]{1,0:T(8,128)(2,1)S(1)}, bf16[24,4096]{1,0:T(8,128)(2,1)S(1)}, u32[]{:S(2)}, u32[]{:S(2)}) collective-permute-start(bf16[24,4096]{1,0:T(8,128)(2,1)S(1)} %get-tuple-element.58), channel_id=1, source_target_pairs={{0,2},{1,3},{2,0},{3,1},{4,6},{5,7},{6,4},{7,5},{8,10},{9,11},{10,... | collective-permute-start | bytes 589832 | tf_op jit(solution)/shard_map/ppermute | solution.py:289
  6.3 26.7 %collective-permute-start.1 = (bf16[24,4096]{1,0:T(8,128)(2,1)S(1)}, bf16[24,4096]{1,0:T(8,128)(2,1)S(1)}, u32[]{:S(2)}, u32[]{:S(2)}) collective-permute-start(bf16[24,4096]{1,0:T(8,128)(2,1)S(1)} %get-tuple-element.59), channel_id=1, source_target_pairs={{0,4},{1,5},{2,6},{3,7},{4,0},{5,1},{6,2},{7,3},{8,12},{9,13},{10,... | collective-permute-start | bytes 589832 | tf_op jit(solution)/shard_map/ppermute | solution.py:289
  8.8 25.8 %collective-permute-start.2 = (bf16[24,4096]{1,0:T(8,128)(2,1)S(1)}, bf16[24,4096]{1,0:T(8,128)(2,1)S(1)}, u32[]{:S(2)}, u32[]{:S(2)}) collective-permute-start(bf16[24,4096]{1,0:T(8,128)(2,1)S(1)} %get-tuple-element.60), channel_id=1, source_target_pairs={{0,6},{1,7},{2,4},{3,5},{4,2},{5,3},{6,0},{7,1},{8,14},{9,15},{10,... | collective-permute-start | bytes 589832 | tf_op jit(solution)/shard_map/ppermute | solution.py:289
  8.8 31.3 %collective-permute-start.3 = (bf16[24,4096]{1,0:T(8,128)(2,1)S(1)}, bf16[24,4096]{1,0:T(8,128)(2,1)S(1)}, u32[]{:S(2)}, u32[]{:S(2)}) collective-permute-start(bf16[24,4096]{1,0:T(8,128)(2,1)S(1)} %get-tuple-element.57.refs_0_.refs_1_), channel_id=1, source_target_pairs={{0,1},{1,0},{2,3},{3,2},{4,5},{5,4},{6,7},{7,6},{8,9},{9,8},{10,11... | collective-permute-start | bytes 589832 | tf_op jit(solution)/shard_map/ppermute | solution.py:294
  14.7 60.0 %copy-start = (bf16[3584,1536]{1,0:T(8,128)(2,1)}, bf16[3584,1536]{1,0:T(8,128)(2,1)S(1)}, u32[]{:S(2)}) copy-start(bf16[3584,1536]{1,0:T(8,128)(2,1)S(1)} %fetch.6.refs_3_.refs_1_.refs_4_) | copy-start | bytes 33030148
  21.7 52.9 %copy-start.3 = (bf16[3584,1024]{1,0:T(8,128)(2,1)}, bf16[3584,1024]{1,0:T(8,128)(2,1)S(1)}, u32[]{:S(2)}) copy-start(bf16[3584,1024]{1,0:T(8,128)(2,1)S(1)} %fetch.7.refs_4_.refs_1_) | copy-start | bytes 22020100
  28.5 4.1 %copy-start.1 = (bf16[3584,1536]{1,0:T(8,128)(2,1)}, bf16[3584,1536]{1,0:T(8,128)(2,1)S(1)}, u32[]{:S(2)}) copy-start(bf16[3584,1536]{1,0:T(8,128)(2,1)S(1)} %fetch.5.refs_1_.refs_3_) | copy-start | bytes 33030148
  32.6 7.8 %collective-permute-start.4 = (bf16[24,4096]{1,0:T(8,128)(2,1)S(1)}, bf16[24,4096]{1,0:T(8,128)(2,1)S(1)}, u32[]{:S(2)}, u32[]{:S(2)}) collective-permute-start(bf16[24,4096]{1,0:T(8,128)(2,1)S(1)} %collective-permute-done.refs_1_), channel_id=1, source_target_pairs={{0,1},{1,0},{2,3},{3,2},{4,5},{5,4},{6,7},{7,6},{8,9},{9,8},{10,11... | collective-permute-start | bytes 589832 | tf_op jit(solution)/shard_map/ppermute | solution.py:294
  32.9 11.6 %collective-permute-start.5 = (bf16[24,4096]{1,0:T(8,128)(2,1)S(1)}, bf16[24,4096]{1,0:T(8,128)(2,1)S(1)}, u32[]{:S(2)}, u32[]{:S(2)}) collective-permute-start(bf16[24,4096]{1,0:T(8,128)(2,1)S(1)} %collective-permute-done.1.refs_2_), channel_id=1, source_target_pairs={{0,1},{1,0},{2,3},{3,2},{4,5},{5,4},{6,7},{7,6},{8,9},{9,8},{10,11... | collective-permute-start | bytes 589832 | tf_op jit(solution)/shard_map/ppermute | solution.py:294
  34.6 12.0 %collective-permute-start.6 = (bf16[24,4096]{1,0:T(8,128)(2,1)S(1)}, bf16[24,4096]{1,0:T(8,128)(2,1)S(1)}, u32[]{:S(2)}, u32[]{:S(2)}) collective-permute-start(bf16[24,4096]{1,0:T(8,128)(2,1)S(1)} %collective-permute-done.2.refs_3_), channel_id=1, source_target_pairs={{0,1},{1,0},{2,3},{3,2},{4,5},{5,4},{6,7},{7,6},{8,9},{9,8},{10,11... | collective-permute-start | bytes 589832 | tf_op jit(solution)/shard_map/ppermute | solution.py:294
  63.8 4.1 %copy-start.2 = (bf16[3584,1536]{1,0:T(8,128)(2,1)S(1)}, bf16[3584,1536]{1,0:T(8,128)(2,1)}, u32[]{:S(2)}) copy-start(bf16[3584,1536]{1,0:T(8,128)(2,1)} %copy-done.1) | copy-start | bytes 33030148
  70.2 9.9 %collective-permute-start.7 = (bf16[96,1536]{1,0:T(8,128)(2,1)S(1)}, bf16[96,1536]{1,0:T(8,128)(2,1)S(1)}, u32[]{:S(2)}, u32[]{:S(2)}) collective-permute-start(bf16[96,1536]{1,0:T(8,128)(2,1)S(1)} %get-tuple-element.64), channel_id=1, source_target_pairs={{0,1},{1,0},{2,3},{3,2},{4,5},{5,4},{6,7},{7,6},{8,9},{9,8},{10,11... | collective-permute-start | bytes 884744 | tf_op jit(solution)/shard_map/ppermute | solution.py:294
  73.1 12.4 %collective-permute-start.12 = (bf16[96,1536]{1,0:T(8,128)(2,1)S(1)}, bf16[96,1536]{1,0:T(8,128)(2,1)S(1)}, u32[]{:S(2)}, u32[]{:S(2)}) collective-permute-start(bf16[96,1536]{1,0:T(8,128)(2,1)S(1)} %get-tuple-element.70), channel_id=1, source_target_pairs={{0,1},{1,0},{2,3},{3,2},{4,5},{5,4},{6,7},{7,6},{8,9},{9,8},{10,11... | collective-permute-start | bytes 884744 | tf_op jit(solution)/shard_map/ppermute | solution.py:294
  74.7 21.0 %copy-start.9 = (f32[1,4096,4]{1,2,0:T(4,128)S(1)}, f32[1,4096,4]{1,2,0:T(4,128)}, u32[]{:S(2)}) copy-start(f32[1,4096,4]{1,2,0:T(4,128)} %param.12) | copy-start | bytes 196612
  74.7 21.5 %copy-start.5 = (bf16[1,32,4096]{2,1,0:T(8,128)(2,1)S(1)}, bf16[1,32,4096]{2,1,0:T(8,128)(2,1)}, u32[]{:S(2)}) copy-start(bf16[1,32,4096]{2,1,0:T(8,128)(2,1)} %param.8) | copy-start | bytes 786436
  74.7 29.5 %copy-start.6 = (bf16[1,32,4096]{2,1,0:T(8,128)(2,1)S(1)}, bf16[1,32,4096]{2,1,0:T(8,128)(2,1)}, u32[]{:S(2)}) copy-start(bf16[1,32,4096]{2,1,0:T(8,128)(2,1)} %param.9) | copy-start | bytes 786436
  74.7 29.5 %copy-start.8 = (f32[1,4096]{1,0:T(1,128)S(1)}, f32[1,4096]{1,0:T(1,128)}, u32[]{:S(2)}) copy-start(f32[1,4096]{1,0:T(1,128)} %refs_4_.1) | copy-start | bytes 49156
  76.3 11.3 %collective-permute-start.17 = (bf16[96,1024]{1,0:T(8,128)(2,1)S(1)}, bf16[96,1024]{1,0:T(8,128)(2,1)S(1)}, u32[]{:S(2)}, u32[]{:S(2)}) collective-permute-start(bf16[96,1024]{1,0:T(8,128)(2,1)S(1)} %get-tuple-element.76), channel_id=1, source_target_pairs={{0,1},{1,0},{2,3},{3,2},{4,5},{5,4},{6,7},{7,6},{8,9},{9,8},{10,11... | collective-permute-start | bytes 589832 | tf_op jit(solution)/shard_map/ppermute | solution.py:294
  80.2 9.5 %collective-permute-start.8 = (bf16[24,1536]{1,0:T(8,128)(2,1)S(1)}, bf16[24,1536]{1,0:T(8,128)(2,1)S(1)}, u32[]{:S(2)}, u32[]{:S(2)}) collective-permute-start(bf16[24,1536]{1,0:T(8,128)(2,1)S(1)} %get-tuple-element.66), channel_id=1, source_target_pairs={{0,2},{1,3},{2,0},{3,1},{4,6},{5,7},{6,4},{7,5},{8,10},{9,11},{10,... | collective-permute-start | bytes 221192 | tf_op jit(solution)/shard_map/ppermute | solution.py:289
  80.9 10.2 %collective-permute-start.9 = (bf16[24,1536]{1,0:T(8,128)(2,1)S(1)}, bf16[24,1536]{1,0:T(8,128)(2,1)S(1)}, u32[]{:S(2)}, u32[]{:S(2)}) collective-permute-start(bf16[24,1536]{1,0:T(8,128)(2,1)S(1)} %get-tuple-element.67), channel_id=1, source_target_pairs={{0,4},{1,5},{2,6},{3,7},{4,0},{5,1},{6,2},{7,3},{8,12},{9,13},{10,... | collective-permute-start | bytes 221192 | tf_op jit(solution)/shard_map/ppermute | solution.py:289
  84.4 7.4 %collective-permute-start.10 = (bf16[24,1536]{1,0:T(8,128)(2,1)S(1)}, bf16[24,1536]{1,0:T(8,128)(2,1)S(1)}, u32[]{:S(2)}, u32[]{:S(2)}) collective-permute-start(bf16[24,1536]{1,0:T(8,128)(2,1)S(1)} %get-tuple-element.68), channel_id=1, source_target_pairs={{0,6},{1,7},{2,4},{3,5},{4,2},{5,3},{6,0},{7,1},{8,14},{9,15},{10,... | collective-permute-start | bytes 221192 | tf_op jit(solution)/shard_map/ppermute | solution.py:289
  85.6 8.6 %collective-permute-start.13 = (bf16[24,1536]{1,0:T(8,128)(2,1)S(1)}, bf16[24,1536]{1,0:T(8,128)(2,1)S(1)}, u32[]{:S(2)}, u32[]{:S(2)}) collective-permute-start(bf16[24,1536]{1,0:T(8,128)(2,1)S(1)} %get-tuple-element.72), channel_id=1, source_target_pairs={{0,2},{1,3},{2,0},{3,1},{4,6},{5,7},{6,4},{7,5},{8,10},{9,11},{10,... | collective-permute-start | bytes 221192 | tf_op jit(solution)/shard_map/ppermute | solution.py:289
  87.6 8.7 %collective-permute-start.14 = (bf16[24,1536]{1,0:T(8,128)(2,1)S(1)}, bf16[24,1536]{1,0:T(8,128)(2,1)S(1)}, u32[]{:S(2)}, u32[]{:S(2)}) collective-permute-start(bf16[24,1536]{1,0:T(8,128)(2,1)S(1)} %get-tuple-element.73), channel_id=1, source_target_pairs={{0,4},{1,5},{2,6},{3,7},{4,0},{5,1},{6,2},{7,3},{8,12},{9,13},{10,... | collective-permute-start | bytes 221192 | tf_op jit(solution)/shard_map/ppermute | solution.py:289
  89.7 6.8 %collective-permute-start.15 = (bf16[24,1536]{1,0:T(8,128)(2,1)S(1)}, bf16[24,1536]{1,0:T(8,128)(2,1)S(1)}, u32[]{:S(2)}, u32[]{:S(2)}) collective-permute-start(bf16[24,1536]{1,0:T(8,128)(2,1)S(1)} %get-tuple-element.74), channel_id=1, source_target_pairs={{0,6},{1,7},{2,4},{3,5},{4,2},{5,3},{6,0},{7,1},{8,14},{9,15},{10,... | collective-permute-start | bytes 221192 | tf_op jit(solution)/shard_map/ppermute | solution.py:289
  91.2 7.1 %collective-permute-start.18 = (bf16[24,1024]{1,0:T(8,128)(2,1)S(1)}, bf16[24,1024]{1,0:T(8,128)(2,1)S(1)}, u32[]{:S(2)}, u32[]{:S(2)}) collective-permute-start(bf16[24,1024]{1,0:T(8,128)(2,1)S(1)} %get-tuple-element.78), channel_id=1, source_target_pairs={{0,2},{1,3},{2,0},{3,1},{4,6},{5,7},{6,4},{7,5},{8,10},{9,11},{10,... | collective-permute-start | bytes 147464 | tf_op jit(solution)/shard_map/ppermute | solution.py:289
  91.8 6.8 %collective-permute-start.19 = (bf16[24,1024]{1,0:T(8,128)(2,1)S(1)}, bf16[24,1024]{1,0:T(8,128)(2,1)S(1)}, u32[]{:S(2)}, u32[]{:S(2)}) collective-permute-start(bf16[24,1024]{1,0:T(8,128)(2,1)S(1)} %get-tuple-element.79), channel_id=1, source_target_pairs={{0,4},{1,5},{2,6},{3,7},{4,0},{5,1},{6,2},{7,3},{8,12},{9,13},{10,... | collective-permute-start | bytes 147464 | tf_op jit(solution)/shard_map/ppermute | solution.py:289
  94.2 5.9 %collective-permute-start.20 = (bf16[24,1024]{1,0:T(8,128)(2,1)S(1)}, bf16[24,1024]{1,0:T(8,128)(2,1)S(1)}, u32[]{:S(2)}, u32[]{:S(2)}) collective-permute-start(bf16[24,1024]{1,0:T(8,128)(2,1)S(1)} %get-tuple-element.80), channel_id=1, source_target_pairs={{0,6},{1,7},{2,4},{3,5},{4,2},{5,3},{6,0},{7,1},{8,14},{9,15},{10,... | collective-permute-start | bytes 147464 | tf_op jit(solution)/shard_map/ppermute | solution.py:289
  96.2 56.1 %slice-start.3 = ((s8[11010048]{0:T(1024)(128)(4,1)}), s8[2621440]{0:T(1024)(128)(4,1)S(1)}, s32[]{:S(2)}) async-start(s8[11010048]{0:T(1024)(128)(4,1)} %bitcast.19), calls=%async_computation.3 | async-start | bytes 5242880
  96.4 7.8 %collective-permute-start.11 = (bf16[32,1536]{1,0:T(8,128)(2,1)S(1)}, bf16[32,1536]{1,0:T(8,128)(2,1)S(1)}, u32[]{:S(2)}, u32[]{:S(2)}) collective-permute-start(bf16[32,1536]{1,0:T(8,128)(2,1)S(1)} %combine.6), channel_id=1, source_target_pairs={{0,8},{8,16},{16,24},{24,0},{1,9},{9,17},{17,25},{25,1},{2,10},{10... | collective-permute-start | bytes 294920 | tf_op jit(solution)/shard_map/ppermute | solution.py:299
  96.6 7.5 %collective-permute-start.16 = (bf16[32,1536]{1,0:T(8,128)(2,1)S(1)}, bf16[32,1536]{1,0:T(8,128)(2,1)S(1)}, u32[]{:S(2)}, u32[]{:S(2)}) collective-permute-start(bf16[32,1536]{1,0:T(8,128)(2,1)S(1)} %combine.7), channel_id=1, source_target_pairs={{0,8},{8,16},{16,24},{24,0},{1,9},{9,17},{17,25},{25,1},{2,10},{10... | collective-permute-start | bytes 294920 | tf_op jit(solution)/shard_map/ppermute | solution.py:299
  100.2 3.9 %collective-permute-start.21 = (bf16[32,1024]{1,0:T(8,128)(2,1)S(1)}, bf16[32,1024]{1,0:T(8,128)(2,1)S(1)}, u32[]{:S(2)}, u32[]{:S(2)}) collective-permute-start(bf16[32,1024]{1,0:T(8,128)(2,1)S(1)} %combine.8), channel_id=1, source_target_pairs={{0,8},{8,16},{16,24},{24,0},{1,9},{9,17},{17,25},{25,1},{2,10},{10... | collective-permute-start | bytes 196616 | tf_op jit(solution)/shard_map/ppermute | solution.py:299
  104.9 9.4 %collective-permute-start.22 = (bf16[24,4096]{1,0:T(8,128)(2,1)S(1)}, bf16[24,4096]{1,0:T(8,128)(2,1)S(1)}, u32[]{:S(2)}, u32[]{:S(2)}) collective-permute-start(bf16[24,4096]{1,0:T(8,128)(2,1)S(1)} %get-tuple-element.84), channel_id=1, source_target_pairs={{0,2},{1,3},{2,0},{3,1},{4,6},{5,7},{6,4},{7,5},{8,10},{9,11},{10,... | collective-permute-start | bytes 589832 | tf_op jit(solution)/shard_map/ppermute | solution.py:289
  105.0 17.2 %collective-permute-start.23 = (bf16[24,4096]{1,0:T(8,128)(2,1)S(1)}, bf16[24,4096]{1,0:T(8,128)(2,1)S(1)}, u32[]{:S(2)}, u32[]{:S(2)}) collective-permute-start(bf16[24,4096]{1,0:T(8,128)(2,1)S(1)} %get-tuple-element.85), channel_id=1, source_target_pairs={{0,4},{1,5},{2,6},{3,7},{4,0},{5,1},{6,2},{7,3},{8,12},{9,13},{10,... | collective-permute-start | bytes 589832 | tf_op jit(solution)/shard_map/ppermute | solution.py:289
  107.0 15.6 %collective-permute-start.24 = (bf16[24,4096]{1,0:T(8,128)(2,1)S(1)}, bf16[24,4096]{1,0:T(8,128)(2,1)S(1)}, u32[]{:S(2)}, u32[]{:S(2)}) collective-permute-start(bf16[24,4096]{1,0:T(8,128)(2,1)S(1)} %get-tuple-element.86), channel_id=1, source_target_pairs={{0,6},{1,7},{2,4},{3,5},{4,2},{5,3},{6,0},{7,1},{8,14},{9,15},{10,... | collective-permute-start | bytes 589832 | tf_op jit(solution)/shard_map/ppermute | solution.py:289
  109.3 14.8 %collective-permute-start.25 = (bf16[24,4096]{1,0:T(8,128)(2,1)S(1)}, bf16[24,4096]{1,0:T(8,128)(2,1)S(1)}, u32[]{:S(2)}, u32[]{:S(2)}) collective-permute-start(bf16[24,4096]{1,0:T(8,128)(2,1)S(1)} %get-tuple-element.83.refs_0_), channel_id=1, source_target_pairs={{0,1},{1,0},{2,3},{3,2},{4,5},{5,4},{6,7},{7,6},{8,9},{9,8},{10,11... | collective-permute-start | bytes 589832 | tf_op jit(solution)/shard_map/ppermute | solution.py:294
  114.3 9.9 %collective-permute-start.26 = (bf16[24,4096]{1,0:T(8,128)(2,1)S(1)}, bf16[24,4096]{1,0:T(8,128)(2,1)S(1)}, u32[]{:S(2)}, u32[]{:S(2)}) collective-permute-start(bf16[24,4096]{1,0:T(8,128)(2,1)S(1)} %collective-permute-done.22.refs_1_), channel_id=1, source_target_pairs={{0,1},{1,0},{2,3},{3,2},{4,5},{5,4},{6,7},{7,6},{8,9},{9,8},{10,11... | collective-permute-start | bytes 589832 | tf_op jit(solution)/shard_map/ppermute | solution.py:294
  122.1 5.7 %collective-permute-start.27 = (bf16[24,4096]{1,0:T(8,128)(2,1)S(1)}, bf16[24,4096]{1,0:T(8,128)(2,1)S(1)}, u32[]{:S(2)}, u32[]{:S(2)}) collective-permute-start(bf16[24,4096]{1,0:T(8,128)(2,1)S(1)} %collective-permute-done.23.refs_2_), channel_id=1, source_target_pairs={{0,1},{1,0},{2,3},{3,2},{4,5},{5,4},{6,7},{7,6},{8,9},{9,8},{10,11... | collective-permute-start | bytes 589832 | tf_op jit(solution)/shard_map/ppermute | solution.py:294
  122.7 7.2 %collective-permute-start.28 = (bf16[24,4096]{1,0:T(8,128)(2,1)S(1)}, bf16[24,4096]{1,0:T(8,128)(2,1)S(1)}, u32[]{:S(2)}, u32[]{:S(2)}) collective-permute-start(bf16[24,4096]{1,0:T(8,128)(2,1)S(1)} %collective-permute-done.24.refs_3_), channel_id=1, source_target_pairs={{0,1},{1,0},{2,3},{3,2},{4,5},{5,4},{6,7},{7,6},{8,9},{9,8},{10,11... | collective-permute-start | bytes 589832 | tf_op jit(solution)/shard_map/ppermute | solution.py:294
  129.9 22.4 %slice-start = ((s8[11010048]{0:T(1024)(128)(4,1)}), s8[4194304]{0:T(1024)(128)(4,1)S(1)}, s32[]{:S(2)}) async-start(s8[11010048]{0:T(1024)(128)(4,1)} %bitcast.17), calls=%async_computation | async-start | bytes 8388608
  129.9 22.4 %slice-start.6 = ((s8[7340032]{0:T(1024)(128)(4,1)}), s8[4194304]{0:T(1024)(128)(4,1)S(1)}, s32[]{:S(2)}) async-start(s8[7340032]{0:T(1024)(128)(4,1)} %bitcast.21), calls=%async_computation.6 | async-start | bytes 8388608
  130.0 22.3 %slice-start.1 = ((s8[11010048]{0:T(1024)(128)(4,1)}), s8[4194304]{0:T(1024)(128)(4,1)S(1)}, s32[]{:S(2)}) async-start(s8[11010048]{0:T(1024)(128)(4,1)} %bitcast.17), calls=%async_computation.1 | async-start | bytes 8388608
  130.0 22.3 %slice-start.2 = ((s8[11010048]{0:T(1024)(128)(4,1)}), s8[2621440]{0:T(1024)(128)(4,1)S(1)}, s32[]{:S(2)}) async-start(s8[11010048]{0:T(1024)(128)(4,1)} %bitcast.17), calls=%async_computation.2 | async-start | bytes 5242880
  130.0 22.3 %slice-start.4 = ((s8[11010048]{0:T(1024)(128)(4,1)}), s8[4194304]{0:T(1024)(128)(4,1)S(1)}, s32[]{:S(2)}) async-start(s8[11010048]{0:T(1024)(128)(4,1)} %bitcast.19), calls=%async_computation.4 | async-start | bytes 8388608
  130.1 22.3 %slice-start.5 = ((s8[11010048]{0:T(1024)(128)(4,1)}), s8[4194304]{0:T(1024)(128)(4,1)S(1)}, s32[]{:S(2)}) async-start(s8[11010048]{0:T(1024)(128)(4,1)} %bitcast.19), calls=%async_computation.5 | async-start | bytes 8388608
  130.1 22.3 %slice-start.7 = ((s8[7340032]{0:T(1024)(128)(4,1)}), s8[3145728]{0:T(1024)(128)(4,1)S(1)}, s32[]{:S(2)}) async-start(s8[7340032]{0:T(1024)(128)(4,1)} %bitcast.21), calls=%async_computation.7 | async-start | bytes 6291456
  154.7 8.4 %collective-permute-start.29 = (bf16[96,1536]{1,0:T(8,128)(2,1)S(1)}, bf16[96,1536]{1,0:T(8,128)(2,1)S(1)}, u32[]{:S(2)}, u32[]{:S(2)}) collective-permute-start(bf16[96,1536]{1,0:T(8,128)(2,1)S(1)} %get-tuple-element.90), channel_id=1, source_target_pairs={{0,1},{1,0},{2,3},{3,2},{4,5},{5,4},{6,7},{7,6},{8,9},{9,8},{10,11... | collective-permute-start | bytes 884744 | tf_op jit(solution)/shard_map/ppermute | solution.py:294
  157.6 19.4 %collective-permute-start.34 = (bf16[96,1536]{1,0:T(8,128)(2,1)S(1)}, bf16[96,1536]{1,0:T(8,128)(2,1)S(1)}, u32[]{:S(2)}, u32[]{:S(2)}) collective-permute-start(bf16[96,1536]{1,0:T(8,128)(2,1)S(1)} %get-tuple-element.96), channel_id=1, source_target_pairs={{0,1},{1,0},{2,3},{3,2},{4,5},{5,4},{6,7},{7,6},{8,9},{9,8},{10,11... | collective-permute-start | bytes 884744 | tf_op jit(solution)/shard_map/ppermute | solution.py:294
  160.8 7.6 %collective-permute-start.39 = (bf16[96,1024]{1,0:T(8,128)(2,1)S(1)}, bf16[96,1024]{1,0:T(8,128)(2,1)S(1)}, u32[]{:S(2)}, u32[]{:S(2)}) collective-permute-start(bf16[96,1024]{1,0:T(8,128)(2,1)S(1)} %get-tuple-element.102), channel_id=1, source_target_pairs={{0,1},{1,0},{2,3},{3,2},{4,5},{5,4},{6,7},{7,6},{8,9},{9,8},{10,11... | collective-permute-start | bytes 589832 | tf_op jit(solution)/shard_map/ppermute | solution.py:294
  163.1 23.4 %collective-permute-start.30 = (bf16[24,1536]{1,0:T(8,128)(2,1)S(1)}, bf16[24,1536]{1,0:T(8,128)(2,1)S(1)}, u32[]{:S(2)}, u32[]{:S(2)}) collective-permute-start(bf16[24,1536]{1,0:T(8,128)(2,1)S(1)} %get-tuple-element.92), channel_id=1, source_target_pairs={{0,2},{1,3},{2,0},{3,1},{4,6},{5,7},{6,4},{7,5},{8,10},{9,11},{10,... | collective-permute-start | bytes 221192 | tf_op jit(solution)/shard_map/ppermute | solution.py:289
  168.4 9.2 %collective-permute-start.40 = (bf16[24,1024]{1,0:T(8,128)(2,1)S(1)}, bf16[24,1024]{1,0:T(8,128)(2,1)S(1)}, u32[]{:S(2)}, u32[]{:S(2)}) collective-permute-start(bf16[24,1024]{1,0:T(8,128)(2,1)S(1)} %get-tuple-element.104), channel_id=1, source_target_pairs={{0,2},{1,3},{2,0},{3,1},{4,6},{5,7},{6,4},{7,5},{8,10},{9,11},{10,... | collective-permute-start | bytes 147464 | tf_op jit(solution)/shard_map/ppermute | solution.py:289
  174.6 10.3 %collective-permute-start.41 = (bf16[24,1024]{1,0:T(8,128)(2,1)S(1)}, bf16[24,1024]{1,0:T(8,128)(2,1)S(1)}, u32[]{:S(2)}, u32[]{:S(2)}) collective-permute-start(bf16[24,1024]{1,0:T(8,128)(2,1)S(1)} %get-tuple-element.105), channel_id=1, source_target_pairs={{0,4},{1,5},{2,6},{3,7},{4,0},{5,1},{6,2},{7,3},{8,12},{9,13},{10,... | collective-permute-start | bytes 147464 | tf_op jit(solution)/shard_map/ppermute | solution.py:289
  174.6 10.3 %collective-permute-start.42 = (bf16[24,1024]{1,0:T(8,128)(2,1)S(1)}, bf16[24,1024]{1,0:T(8,128)(2,1)S(1)}, u32[]{:S(2)}, u32[]{:S(2)}) collective-permute-start(bf16[24,1024]{1,0:T(8,128)(2,1)S(1)} %get-tuple-element.106), channel_id=1, source_target_pairs={{0,6},{1,7},{2,4},{3,5},{4,2},{5,3},{6,0},{7,1},{8,14},{9,15},{10,... | collective-permute-start | bytes 147464 | tf_op jit(solution)/shard_map/ppermute | solution.py:289
  177.0 13.0 %collective-permute-start.31 = (bf16[24,1536]{1,0:T(8,128)(2,1)S(1)}, bf16[24,1536]{1,0:T(8,128)(2,1)S(1)}, u32[]{:S(2)}, u32[]{:S(2)}) collective-permute-start(bf16[24,1536]{1,0:T(8,128)(2,1)S(1)} %get-tuple-element.93), channel_id=1, source_target_pairs={{0,4},{1,5},{2,6},{3,7},{4,0},{5,1},{6,2},{7,3},{8,12},{9,13},{10,... | collective-permute-start | bytes 221192 | tf_op jit(solution)/shard_map/ppermute | solution.py:289
  177.6 12.5 %collective-permute-start.32 = (bf16[24,1536]{1,0:T(8,128)(2,1)S(1)}, bf16[24,1536]{1,0:T(8,128)(2,1)S(1)}, u32[]{:S(2)}, u32[]{:S(2)}) collective-permute-start(bf16[24,1536]{1,0:T(8,128)(2,1)S(1)} %get-tuple-element.94), channel_id=1, source_target_pairs={{0,6},{1,7},{2,4},{3,5},{4,2},{5,3},{6,0},{7,1},{8,14},{9,15},{10,... | collective-permute-start | bytes 221192 | tf_op jit(solution)/shard_map/ppermute | solution.py:289
  184.9 6.0 %collective-permute-start.35 = (bf16[24,1536]{1,0:T(8,128)(2,1)S(1)}, bf16[24,1536]{1,0:T(8,128)(2,1)S(1)}, u32[]{:S(2)}, u32[]{:S(2)}) collective-permute-start(bf16[24,1536]{1,0:T(8,128)(2,1)S(1)} %get-tuple-element.98), channel_id=1, source_target_pairs={{0,2},{1,3},{2,0},{3,1},{4,6},{5,7},{6,4},{7,5},{8,10},{9,11},{10,... | collective-permute-start | bytes 221192 | tf_op jit(solution)/shard_map/ppermute | solution.py:289
  184.9 6.0 %collective-permute-start.36 = (bf16[24,1536]{1,0:T(8,128)(2,1)S(1)}, bf16[24,1536]{1,0:T(8,128)(2,1)S(1)}, u32[]{:S(2)}, u32[]{:S(2)}) collective-permute-start(bf16[24,1536]{1,0:T(8,128)(2,1)S(1)} %get-tuple-element.99), channel_id=1, source_target_pairs={{0,4},{1,5},{2,6},{3,7},{4,0},{5,1},{6,2},{7,3},{8,12},{9,13},{10,... | collective-permute-start | bytes 221192 | tf_op jit(solution)/shard_map/ppermute | solution.py:289
  186.5 6.2 %collective-permute-start.37 = (bf16[24,1536]{1,0:T(8,128)(2,1)S(1)}, bf16[24,1536]{1,0:T(8,128)(2,1)S(1)}, u32[]{:S(2)}, u32[]{:S(2)}) collective-permute-start(bf16[24,1536]{1,0:T(8,128)(2,1)S(1)} %get-tuple-element.100), channel_id=1, source_target_pairs={{0,6},{1,7},{2,4},{3,5},{4,2},{5,3},{6,0},{7,1},{8,14},{9,15},{10,... | collective-permute-start | bytes 221192 | tf_op jit(solution)/shard_map/ppermute | solution.py:289
  190.0 3.7 %collective-permute-start.43 = (bf16[32,1024]{1,0:T(8,128)(2,1)S(1)}, bf16[32,1024]{1,0:T(8,128)(2,1)S(1)}, u32[]{:S(2)}, u32[]{:S(2)}) collective-permute-start(bf16[32,1024]{1,0:T(8,128)(2,1)S(1)} %combine.11), channel_id=1, source_target_pairs={{0,8},{8,16},{16,24},{24,0},{1,9},{9,17},{17,25},{25,1},{2,10},{10... | collective-permute-start | bytes 196616 | tf_op jit(solution)/shard_map/ppermute | solution.py:299
  190.3 4.5 %collective-permute-start.33 = (bf16[32,1536]{1,0:T(8,128)(2,1)S(1)}, bf16[32,1536]{1,0:T(8,128)(2,1)S(1)}, u32[]{:S(2)}, u32[]{:S(2)}) collective-permute-start(bf16[32,1536]{1,0:T(8,128)(2,1)S(1)} %combine.9), channel_id=1, source_target_pairs={{0,8},{8,16},{16,24},{24,0},{1,9},{9,17},{17,25},{25,1},{2,10},{10... | collective-permute-start | bytes 294920 | tf_op jit(solution)/shard_map/ppermute | solution.py:299
  192.9 4.1 %collective-permute-start.38 = (bf16[32,1536]{1,0:T(8,128)(2,1)S(1)}, bf16[32,1536]{1,0:T(8,128)(2,1)S(1)}, u32[]{:S(2)}, u32[]{:S(2)}) collective-permute-start(bf16[32,1536]{1,0:T(8,128)(2,1)S(1)} %combine.10), channel_id=1, source_target_pairs={{0,8},{8,16},{16,24},{24,0},{1,9},{9,17},{17,25},{25,1},{2,10},{10... | collective-permute-start | bytes 294920 | tf_op jit(solution)/shard_map/ppermute | solution.py:299
